TPU v7x, 32 devices: a whole 2x2x4 slice. The times are simulated.
32 devices in a mesh: dom: 32 (over z, y, x, core).
Axes of the slice: x: 2, y: 2, z: 4, core: 2. Of those that a mesh axis runs over, the one named last changes fastest.
Arguments:
- features: bfloat16 [524288, 256], P('dom'), may hold values from -48 to 48, as said below
- w_first: bfloat16 [1280, 256], replicated, may hold values from -0.15625 to 0.15625
- w_second: bfloat16 [1280, 256], replicated, may hold values from -0.15625 to 0.15625
- seed_owner: int32 [9216, 1], P('dom'), may hold values from 0 to 31; in each aligned block of 288 rows (0 to 287, 288 to 575, ...) at most 18 rows name the same one
- seed_row: int32 [9216], P('dom'), may hold values from 0 to 16383
- hop1_owner: int32 [36864, 1], P('dom'), may hold values from 0 to 31; in each aligned block of 1152 rows (0 to 1151, 1152 to 2303, ...) at most 72 rows name the same one
- hop1_row: int32 [36864], P('dom'), may hold values from 0 to 16383
- hop1_rel: int32 [36864], P('dom'), may hold values from 0 to 3
- hop2_owner: int32 [73728, 1], P('dom'), may hold values from 0 to 31; in each aligned block of 2304 rows (0 to 2303, 2304 to 4607, ...) at most 144 rows name the same one
- hop2_row: int32 [73728], P('dom'), may hold values from 0 to 16383
- hop2_rel: int32 [73728], P('dom'), may hold values from 0 to 3
- edge_mask: int32 [4096], P('dom'), may hold values 0 or 1
Outputs:
- edge_loss: float32 [4096], P('dom')
- mean_loss: float32 [], replicated
Inputs may be any that keep to these rules, and one draw needn't show every extreme that they name: `features`: standard normal entries; in some draws each row is scaled by a factor up to 10. `seed_owner`: among the rows of one device no owner is named by more than 18 rows; some owner is named by exactly 18 in every draw. `hop1_owner`: among the rows of one device no owner is named by more than 72 rows; some owner is named by exactly 72 in every draw. `hop2_owner`: among the rows of one device no owner is named by more than 144 rows; some owner is named by exactly 144 in every draw.
All inputs are finite; a program needn't handle non-finite values. No bound on the sum of `edge_mask` on one device may be relied on, other than what follows from the above.
Results may differ from a plain program's by a relative error of at most 0.002.
Values may be sent and summed in bfloat16 or wider, within the bound.
A program may use at most 64 MiB of HBM per device.

v0:
```python
import jax
import jax.numpy as jnp
from jax import lax
from jax.sharding import PartitionSpec as P

R = 4
BLOCK = 128
NEG = 32
FAN1 = 4
FAN2 = 2


def bucket_rows(owner, rows, devices, capacity):
    owners = owner[:, 0]
    length = owners.shape[0]
    onehot = (owners[:, None] == jnp.arange(devices, dtype=jnp.int32)[None, :]).astype(jnp.bfloat16)
    counter = jnp.arange(length, dtype=jnp.int32)
    earlier = (counter[:, None] > counter[None, :]).astype(jnp.bfloat16)
    prior = jnp.dot(earlier, onehot, preferred_element_type=jnp.float32)
    position = jnp.sum(prior * onehot.astype(jnp.float32), axis=1).astype(jnp.int32)
    slot_index = owners * capacity + position
    slot_hot = (
        slot_index[:, None] == jnp.arange(devices * capacity, dtype=jnp.int32)[None, :]
    ).astype(jnp.bfloat16)
    halves = jnp.stack([rows // 128, rows % 128], axis=1).astype(jnp.bfloat16)
    placed = lax.dot_general(
        slot_hot, halves, (((0,), (0,)), ((), ())), preferred_element_type=jnp.float32
    )
    requests = (placed[:, 0] * 128.0 + placed[:, 1]).astype(jnp.int32)
    return (slot_index, requests.reshape(devices, capacity))


def unpack_rows(returned, slot_index):
    return returned[slot_index]


def fetch_apart(owner, rows, features, devices):
    capacity = (2 * owner.shape[0] + devices - 1) // devices
    slot_index, requests = bucket_rows(owner, rows, devices, capacity)
    arrived = lax.all_to_all(requests, "dom", split_axis=0, concat_axis=0, tiled=True)
    located = features[arrived.reshape(-1)].reshape(devices, capacity, features.shape[1])
    returned = lax.all_to_all(located, "dom", split_axis=0, concat_axis=0, tiled=True)
    return unpack_rows(returned.reshape(devices * capacity, features.shape[1]), slot_index)


def rgcn_layer(self_rows, neighbours, relations, weights):
    width = self_rows.shape[1]
    onehot = (relations[..., None] == jnp.arange(R, dtype=jnp.int32)).astype(jnp.float32)
    tallies = jnp.maximum(jnp.sum(onehot, axis=1), 1.0)
    shares = onehot / tallies[:, None, :]
    merged = shares[:, 0, :, None] * neighbours[:, 0, None, :].astype(jnp.float32)
    for column in range(1, neighbours.shape[1]):
        merged = merged + shares[:, column, :, None] * neighbours[:, column, None, :].astype(
            jnp.float32
        )
    merged = merged.astype(jnp.bfloat16).reshape(self_rows.shape[0], R * width)
    inputs = jnp.concatenate([self_rows, merged], axis=1)
    return jnp.dot(inputs, weights, preferred_element_type=jnp.float32)


def shards(
    features,
    w_first,
    w_second,
    seed_owner,
    seed_row,
    hop1_owner,
    hop1_row,
    hop1_rel,
    hop2_owner,
    hop2_row,
    hop2_rel,
    edge_mask,
):
    devices = lax.axis_size("dom")
    width = features.shape[1]
    seed_count = seed_row.shape[0]
    first_count = hop1_row.shape[0]
    positives = edge_mask.shape[0]
    blocks = positives // BLOCK
    x_hop2 = fetch_apart(hop2_owner, hop2_row, features, devices)
    x_hop1 = fetch_apart(hop1_owner, hop1_row, features, devices)
    x_seed = fetch_apart(seed_owner, seed_row, features, devices)
    first_hop = jax.nn.relu(
        rgcn_layer(
            x_hop1,
            x_hop2.reshape(first_count, FAN2, width),
            hop2_rel.reshape(first_count, FAN2),
            w_first,
        )
    ).astype(jnp.bfloat16)
    first_seed = jax.nn.relu(
        rgcn_layer(
            x_seed,
            x_hop1.reshape(seed_count, FAN1, width),
            hop1_rel.reshape(seed_count, FAN1),
            w_first,
        )
    ).astype(jnp.bfloat16)
    second = rgcn_layer(
        first_seed,
        first_hop.reshape(seed_count, FAN1, width),
        hop1_rel.reshape(seed_count, FAN1),
        w_second,
    )
    sources = second[:positives]
    targets = second[positives : 2 * positives]
    negatives = second[2 * positives :].reshape(blocks, NEG, width)
    positive = jnp.sum(sources * targets, axis=1)
    negative = jnp.einsum(
        "bef,bqf->beq",
        sources.reshape(blocks, BLOCK, width),
        negatives,
        precision=lax.Precision.HIGHEST,
    ).reshape(positives, NEG)
    scores = jnp.concatenate([positive[:, None], negative], axis=1)
    top_score = jnp.max(scores, axis=1, keepdims=True)
    edge_loss = top_score[:, 0] + jnp.log(jnp.sum(jnp.exp(scores - top_score), axis=1)) - positive
    weights = edge_mask.astype(jnp.float32)
    loss_total, edge_total = lax.psum((jnp.sum(weights * edge_loss), jnp.sum(weights)), "dom")
    mean_loss = loss_total / jnp.maximum(edge_total, 1.0)
    return (edge_loss, mean_loss)


def solution(mesh):
    placed = (
        P("dom", None),
        P(),
        P(),
        P("dom", None),
        P("dom"),
        P("dom", None),
        P("dom"),
        P("dom"),
        P("dom", None),
        P("dom"),
        P("dom"),
        P("dom"),
    )
    return jax.shard_map(
        shards, mesh=mesh, in_specs=placed, out_specs=(P("dom"), P()), check_vma=False
    )
```

profile of v0, /device:TPU:0, one launch (start us, length us, event | category | flops | bytes accessed | tf_op | source)
XLA Modules:
  0.0 227.9 jit_solution(11600786799563126268)
XLA Ops:
  0.6 0.8 reduce.2
  1.4 0.2 fusion.21
  1.6 0.7 fusion.71
  2.3 0.7 fusion.68
  3.0 0.3 fusion.29
  3.4 0.7 convert_element_type.153
  4.1 7.3 %all-to-all-start = ((s32[32,1,18]{2,1,0:T(1,128)}), s32[32,1,18]{2,1,0:T(1,128)S(1)}, u32[]{:S(2)}, u32[]{:S(2)}) async-start(s32[32,1,18]{2,1,0:T(1,128)} %bitcast), calls=%async_computation | async-start | bytes 32768 | tf_op jit(solution)/shard_map/all_to_all | solution.py:40
  11.4 0.7 reduce.14
  12.2 1.9 fusion.19
  14.2 7.4 %fusion = f32[4608,2]{0,1:T(2,128)S(1)} fusion(s32[2304]{0:T(1024)S(1)} %get-tuple-element.3, bf16[2304,1]{0,1:T(2,128)(2,1)S(1)} %stack.43, bf16[2304,1]{0,1:T(2,128)(2,1)S(1)} %stack.42), kind=kOutput, calls=%fused_computation.7 | convolution fusion | flops 53102592 | bytes 55296 | tf_op jit(solution)/shard_map/dot_general | solution.py:26
  21.7 0.6 fusion.20
  22.5 2.0 fusion.3
  24.5 0.7 convert_element_type.173
  25.2 0.7 convert_element_type.160
  25.9 6.0 %all-to-all-start.2 = ((s32[32,1,72]{2,1,0:T(1,128)}), s32[32,1,72]{2,1,0:T(1,128)S(1)}, u32[]{:S(2)}, u32[]{:S(2)}) async-start(s32[32,1,72]{2,1,0:T(1,128)} %bitcast.2), calls=%async_computation.2 | async-start | bytes 32768 | tf_op jit(solution)/shard_map/all_to_all | solution.py:40
  31.9 0.5 broadcast.221
  32.4 0.7 reduce.37
  33.3 5.7 %all-to-all-done.2 = s32[32,1,72]{2,1,0:T(1,128)S(1)} async-done(((s32[32,1,72]{2,1,0:T(1,128)}), s32[32,1,72]{2,1,0:T(1,128)S(1)}, u32[]{:S(2)}, u32[]{:S(2)}) %all-to-all-start.2) | async-done | bytes 9248 | tf_op jit(solution)/shard_map/all_to_all | solution.py:40
  38.9 2.6 %all-to-all-start.4 = ((s32[32,1,144]{2,1,0:T(1,128)}), s32[32,1,144]{2,1,0:T(1,128)S(1)}, u32[]{:S(2)}, u32[]{:S(2)}) async-start(s32[32,1,144]{2,1,0:T(1,128)} %convert_element_type.173), calls=%async_computation.4 | async-start | bytes 65536 | tf_op jit(solution)/shard_map/all_to_all | solution.py:40
  41.5 6.6 %gather_fusion = bf16[576,256]{1,0:T(8,128)(2,1)S(1)} fusion(bf16[16384,256]{1,0:T(8,128)(2,1)} %param.12, s32[1024]{0:T(1024)S(1)} %pad_clamp_fusion.5), kind=kCustom, calls=%fused_computation | custom fusion | bytes 592128 | tf_op jit(solution)/shard_map/gather | solution.py:41
  48.1 0.8 reshape.323
  49.0 5.8 %all-to-all-start.1 = ((bf16[32,18,256]{2,1,0:T(8,128)(2,1)}), bf16[32,18,256]{2,1,0:T(8,128)(2,1)S(1)}, u32[]{:S(2)}, u32[]{:S(2)}) async-start(bf16[32,18,256]{2,1,0:T(8,128)(2,1)} %reshape.323), calls=%async_computation.1 | async-start | bytes 786432 | tf_op jit(solution)/shard_map/all_to_all | solution.py:42
  54.8 0.7 reduce.36
  55.7 10.7 %gather_fusion.2 = bf16[2304,256]{1,0:T(8,128)(2,1)} fusion(bf16[16384,256]{1,0:T(8,128)(2,1)} %param.12, s32[3072]{0:T(1024)S(1)} %pad_clamp_fusion.2), kind=kCustom, calls=%fused_computation.2 | custom fusion | bytes 2368512 | tf_op jit(solution)/shard_map/gather | solution.py:41
  66.4 1.7 all-to-all-done.1
  68.1 0.8 copy-done.5
  68.8 4.1 %all-to-all-start.3 = ((bf16[32,72,256]{2,1,0:T(8,128)(2,1)}), bf16[32,72,256]{2,1,0:T(8,128)(2,1)S(1)}, u32[]{:S(2)}, u32[]{:S(2)}) async-start(bf16[32,72,256]{2,1,0:T(8,128)(2,1)} %bitcast.3), calls=%async_computation.3 | async-start | bytes 2359296 | tf_op jit(solution)/shard_map/all_to_all | solution.py:42
  73.2 15.8 %gather_fusion.4 = bf16[4608,256]{1,0:T(8,128)(2,1)} fusion(bf16[16384,256]{1,0:T(8,128)(2,1)} %param.12, s32[5120]{0:T(1024)S(1)} %pad_clamp_fusion), kind=kCustom, calls=%fused_computation.4 | custom fusion | bytes 4737024 | tf_op jit(solution)/shard_map/gather | solution.py:41
  89.1 12.9 %all-to-all-done.3 = bf16[32,72,256]{2,1,0:T(8,128)(2,1)S(1)} async-done(((bf16[32,72,256]{2,1,0:T(8,128)(2,1)}), bf16[32,72,256]{2,1,0:T(8,128)(2,1)S(1)}, u32[]{:S(2)}, u32[]{:S(2)}) %all-to-all-start.3) | async-done | bytes 1179680 | tf_op jit(solution)/shard_map/all_to_all | solution.py:42
  102.0 1.0 copy-done.1
  103.0 3.6 %all-to-all-start.5 = ((bf16[32,144,256]{2,1,0:T(8,128)(2,1)}), bf16[32,144,256]{2,1,0:T(8,128)(2,1)S(1)}, u32[]{:S(2)}, u32[]{:S(2)}) async-start(bf16[32,144,256]{2,1,0:T(8,128)(2,1)} %bitcast.54), calls=%async_computation.5 | async-start | bytes 4718592 | tf_op jit(solution)/shard_map/all_to_all | solution.py:42
  106.6 1.4 eq.153
  108.0 1.3 copy.24
  109.4 1.1 copy.25
  110.4 1.1 copy.27
  112.0 0.8 copy.21
  112.8 0.8 copy.22
  113.6 0.8 copy.23
  114.4 1.1 reshape.324
  115.5 2.5 %gather_fusion.1 = bf16[288,256]{1,0:T(8,128)(2,1)} fusion(bf16[576,256]{1,0:T(8,128)(2,1)S(1)} %reshape.324, s32[1024]{0:T(1024)S(1)} %pad_clamp_fusion.4), kind=kCustom, calls=%fused_computation.1 | custom fusion | bytes 296064 | tf_op jit(solution)/shard_map/gather | solution.py:34
  118.1 5.4 %gather_fusion.3 = bf16[1152,256]{1,0:T(8,128)(2,1)} fusion(bf16[2304,256]{1,0:T(8,128)(2,1)} %bitcast.53, s32[2048]{0:T(1024)S(1)} %pad_clamp_fusion.3), kind=kCustom, calls=%fused_computation.3 | custom fusion | bytes 1184256 | tf_op jit(solution)/shard_map/gather | solution.py:34
  123.4 2.3 reshape.328
  125.7 2.9 %slice_convert_fusion.9 = (f32[288,1,256]{2,1,0:T(1,128)S(1)}, f32[288,1,256]{2,1,0:T(1,128)S(1)}, f32[288,1,256]{2,1,0:T(1,128)S(1)}, f32[288,1,256]{2,1,0:T(1,128)S(1)}) fusion(bf16[288,4,256]{2,1,0:T(4,128)(2,1)} %reshape.328), kind=kLoop, calls=%fused_computation.55 | loop fusion | flops 294912 | bytes 1769472 | tf_op jit(solution)/shard_map/mul | solution.py:51
  128.6 0.8 copy_bitcast_fusion.8
  129.4 0.9 copy_bitcast_fusion.6
  130.3 30.7 %all-to-all-done.5 = bf16[32,144,256]{2,1,0:T(8,128)(2,1)S(1)} async-done(((bf16[32,144,256]{2,1,0:T(8,128)(2,1)}), bf16[32,144,256]{2,1,0:T(8,128)(2,1)S(1)}, u32[]{:S(2)}, u32[]{:S(2)}) %all-to-all-start.5) | async-done | bytes 2359328 | tf_op jit(solution)/shard_map/all_to_all | solution.py:42
  161.0 7.4 %gather_fusion.5 = bf16[2304,256]{1,0:T(8,128)(2,1)} fusion(bf16[4608,256]{1,0:T(8,128)(2,1)S(1)} %bitcast.52, s32[3072]{0:T(1024)S(1)} %pad_clamp_fusion.1), kind=kCustom, calls=%fused_computation.5 | custom fusion | bytes 2368512 | tf_op jit(solution)/shard_map/gather | solution.py:34
  168.4 2.9 %reshape.332 = bf16[1152,2,256]{2,1,0:T(2,128)(2,1)S(1)} reshape(bf16[2304,256]{1,0:T(8,128)(2,1)} %gather_fusion.5) | data formatting | bytes 2359296 | tf_op jit(solution)/shard_map/reshape | solution.py:87
  171.3 1.7 slice_convert_fusion.1
  173.2 0.9 copy-done.2
  174.1 0.2 copy-done.3
  174.2 3.3 %add_convert_fusion = bf16[1152,4,256]{2,1,0:T(4,128)(2,1)S(1)} fusion(f32[1152,256]{1,0:T(8,128)S(1)} %get-tuple-element.43, f32[1152,4]{1,0:T(8,128)S(1)} %copy-done.3, f32[1152,256]{1,0:T(8,128)S(1)} %get-tuple-element.44, f32[1152,4]{1,0:T(8,128)S(1)} %copy-done.2), kind=kLoop, calls=%fused_computation.16 | loop fusion | flops 4718592 | bytes 4755456 | tf_op jit(solution)/shard_map/convert_element_type | solution.py:56
  177.5 0.6 copy.39
  178.1 0.5 copy-done.4
  178.6 1.0 fusion.14
  179.7 0.8 slice_convert_fusion.5
  180.7 0.8 copy-done.6
  181.8 2.0 add_convert_fusion.2
  184.1 0.7 copy-done.12
  184.7 0.4 fusion.18
  185.2 0.4 fusion.25
  185.5 0.3 fusion.84
  186.0 1.2 convert_reduce_fusion.2
  187.2 38.4 %all-reduce = (f32[]{:T(128)}, f32[]{:T(128)}) all-reduce(f32[]{:T(128)} %get-tuple-element.9, f32[]{:T(128)} %get-tuple-element.8), channel_id=1, replica_groups=mesh['dom'=32] {'dom'}, use_global_device_ids=true, to_apply=%region_9.10 | all-reduce | flops 2 | bytes 16 | tf_op jit(solution)/shard_map/psum | solution.py:120
  (89 shorter events, 2.5 us)
Async XLA Ops:
  0.6 177.5 %copy-start = (bf16[1280,256]{1,0:T(8,128)(2,1)S(1)}, bf16[1280,256]{1,0:T(8,128)(2,1)}, u32[]{:S(2)}) copy-start(bf16[1280,256]{1,0:T(8,128)(2,1)} %param.13) | copy-start | bytes 1966084
  4.1 21.8 %all-to-all-start = ((s32[32,1,18]{2,1,0:T(1,128)}), s32[32,1,18]{2,1,0:T(1,128)S(1)}, u32[]{:S(2)}, u32[]{:S(2)}) async-start(s32[32,1,18]{2,1,0:T(1,128)} %bitcast), calls=%async_computation | async-start | bytes 32768 | tf_op jit(solution)/shard_map/all_to_all | solution.py:40
  12.1 1.9 copy-start.13
  12.1 2.0 copy-start.15
  14.2 7.5 %copy-start.14 = (s32[1152,1]{0,1:T(1,128)S(1)}, s32[1152,1]{0,1:T(1,128)}, u32[]{:S(2)}) copy-start(s32[1152,1]{0,1:T(1,128)} %param.17) | copy-start | bytes 13828
  21.6 0.8 copy-start.18
  25.9 13.0 %all-to-all-start.2 = ((s32[32,1,72]{2,1,0:T(1,128)}), s32[32,1,72]{2,1,0:T(1,128)S(1)}, u32[]{:S(2)}, u32[]{:S(2)}) async-start(s32[32,1,72]{2,1,0:T(1,128)} %bitcast.2), calls=%async_computation.2 | async-start | bytes 32768 | tf_op jit(solution)/shard_map/all_to_all | solution.py:40
  38.9 10.0 %all-to-all-start.4 = ((s32[32,1,144]{2,1,0:T(1,128)}), s32[32,1,144]{2,1,0:T(1,128)S(1)}, u32[]{:S(2)}, u32[]{:S(2)}) async-start(s32[32,1,144]{2,1,0:T(1,128)} %convert_element_type.173), calls=%async_computation.4 | async-start | bytes 65536 | tf_op jit(solution)/shard_map/all_to_all | solution.py:40
  49.0 19.1 %all-to-all-start.1 = ((bf16[32,18,256]{2,1,0:T(8,128)(2,1)}), bf16[32,18,256]{2,1,0:T(8,128)(2,1)S(1)}, u32[]{:S(2)}, u32[]{:S(2)}) async-start(bf16[32,18,256]{2,1,0:T(8,128)(2,1)} %reshape.323), calls=%async_computation.1 | async-start | bytes 786432 | tf_op jit(solution)/shard_map/all_to_all | solution.py:42
  68.1 0.8 copy-start.5
  68.8 33.2 %all-to-all-start.3 = ((bf16[32,72,256]{2,1,0:T(8,128)(2,1)}), bf16[32,72,256]{2,1,0:T(8,128)(2,1)S(1)}, u32[]{:S(2)}, u32[]{:S(2)}) async-start(bf16[32,72,256]{2,1,0:T(8,128)(2,1)} %bitcast.3), calls=%async_computation.3 | async-start | bytes 2359296 | tf_op jit(solution)/shard_map/all_to_all | solution.py:42
  102.0 1.0 copy-start.1
  102.0 4.6 %copy-start.16 = (s32[2304]{0:T(1024)S(1)}, s32[2304]{0:T(1024)}, u32[]{:S(2)}) copy-start(s32[2304]{0:T(1024)} %param.22) | copy-start | bytes 27652
  103.0 58.0 %all-to-all-start.5 = ((bf16[32,144,256]{2,1,0:T(8,128)(2,1)}), bf16[32,144,256]{2,1,0:T(8,128)(2,1)S(1)}, u32[]{:S(2)}, u32[]{:S(2)}) async-start(bf16[32,144,256]{2,1,0:T(8,128)(2,1)} %bitcast.54), calls=%async_computation.5 | async-start | bytes 4718592 | tf_op jit(solution)/shard_map/all_to_all | solution.py:42
  106.6 4.9 %copy-start.17 = (s32[1152]{0:T(1024)S(1)}, s32[1152]{0:T(1024)}, u32[]{:S(2)}) copy-start(s32[1152]{0:T(1024)} %param.19) | copy-start | bytes 13828
  173.0 1.1 copy-start.2
  173.0 1.2 copy-start.3
  177.5 1.1 copy-start.4
  180.5 1.0 copy-start.6
  180.5 1.0 copy-start.7
  180.5 1.1 copy-start.8
  180.6 1.2 copy-start.9
  180.6 1.2 copy-start.10
  180.6 1.2 copy-start.11
  183.8 0.9 copy-start.12
  184.1 1.1 copy-start.20
  185.2 0.8 copy-start.19
where the time goes:
time: 229 us; the launch traced here: 228 us
  local copies, waits for them, and re-layouts  74 us (32%)
  waiting for transfers between devices  51 us (22%)
  blocking collectives  38.4 us (17%)
  starting transfers between devices  29.5 us (13%)
  other arithmetic  17 us (7%)
  matrix products  14.3 us (6%)
  between operations  3.68 us (2%)
    all_to_all x3, waiting for transfers between devices, fetch_apart(): lax.all_to_all(located, 'dom', split_axis=0, concat_axis=0, tiled=True)  45.4 us
    psum x1, blocking collectives, shards(): lax.psum((jnp.sum(weights * edge_loss), jnp.sum(weights)), 'dom')  38.4 us
    gather x3, local copies, waits for them, and re-layouts, fetch_apart(): features[arrived.reshape(-1)].reshape(devices, capacity, features.shape[1])  33.1 us
    all_to_all x3, starting transfers between devices, fetch_apart(): lax.all_to_all(requests, 'dom', split_axis=0, concat_axis=0, tiled=True)  15.9 us
    gather x3, local copies, waits for them, and re-layouts, unpack_rows(): return returned[slot_index]  15.3 us
    all_to_all x3, starting transfers between devices, fetch_apart(): lax.all_to_all(located, 'dom', split_axis=0, concat_axis=0, tiled=True)  13.6 us
    dot_general x3, matrix products, bucket_rows(): lax.dot_general(slot_hot, halves, (((0,), (0,)), ((), ())), preferred_ele...  9.68 us
    unnamed x52, local copies, waits for them, and re-layouts  7.83 us
  transfers between devices with their start and end apart: 6, of which 4 were waited for; matrix products, arithmetic and copies ran while one was open for 33% of the time, Pallas kernels for 0%

commit v1 on v0

--- a/solution.py
+++ b/solution.py
@@ -1,5 +1,6 @@
 import jax
 import jax.numpy as jnp
+import numpy as np
 from jax import lax
 from jax.sharding import PartitionSpec as P
 
@@ -10,37 +11,48 @@
 FAN2 = 2
 
 
-def bucket_rows(owner, rows, devices, capacity):
-    owners = owner[:, 0]
-    length = owners.shape[0]
-    onehot = (owners[:, None] == jnp.arange(devices, dtype=jnp.int32)[None, :]).astype(jnp.bfloat16)
-    counter = jnp.arange(length, dtype=jnp.int32)
+def bucket_all(owners, rows, group, sets, caps, devices):
+    blocks = owners.shape[0] // group
+    onehot = owners[:, None] == jnp.arange(devices, dtype=jnp.int32)[None, :]
+    hot = onehot.astype(jnp.bfloat16).reshape(blocks, group, devices)
+    counter = jnp.arange(group, dtype=jnp.int32)
     earlier = (counter[:, None] > counter[None, :]).astype(jnp.bfloat16)
-    prior = jnp.dot(earlier, onehot, preferred_element_type=jnp.float32)
-    position = jnp.sum(prior * onehot.astype(jnp.float32), axis=1).astype(jnp.int32)
-    slot_index = owners * capacity + position
-    slot_hot = (
-        slot_index[:, None] == jnp.arange(devices * capacity, dtype=jnp.int32)[None, :]
-    ).astype(jnp.bfloat16)
-    halves = jnp.stack([rows // 128, rows % 128], axis=1).astype(jnp.bfloat16)
-    placed = lax.dot_general(
-        slot_hot, halves, (((0,), (0,)), ((), ())), preferred_element_type=jnp.float32
+    prior = jnp.einsum("ij,bjd->bid", earlier, hot, preferred_element_type=jnp.float32)
+    totals = jnp.sum(hot.astype(jnp.float32), axis=1)
+    carry = []
+    start = 0
+    for count in sets:
+        running = jnp.zeros((devices,), jnp.float32)
+        for block in range(start, start + count):
+            carry.append(running)
+            running = running + totals[block]
+        start += count
+    prior = prior + jnp.stack(carry)[:, None, :]
+    position = jnp.sum(prior * hot.astype(jnp.float32), axis=2).astype(jnp.int32)
+    offsets = np.concatenate([[0], np.cumsum(caps)[:-1]])
+    offset = jnp.asarray(np.repeat(offsets, sets), jnp.int32)
+    capacity = jnp.asarray(np.repeat(np.asarray(caps), sets), jnp.int32)
+    slots = owners.reshape(blocks, group) * capacity[:, None] + position
+    place = (position + offset[:, None]).reshape(-1)
+    width = sum(caps)
+    placed = (place[:, None] == jnp.arange(width, dtype=jnp.int32)[None, :]).astype(jnp.bfloat16)
+    high = jnp.where(onehot, (rows // 128)[:, None], 0).astype(jnp.bfloat16)
+    low = jnp.where(onehot, (rows % 128)[:, None], 0).astype(jnp.bfloat16)
+    digits = lax.dot_general(
+        jnp.concatenate([high, low], axis=1),
+        placed,
+        (((0,), (0,)), ((), ())),
+        preferred_element_type=jnp.float32,
     )
-    requests = (placed[:, 0] * 128.0 + placed[:, 1]).astype(jnp.int32)
-    return (slot_index, requests.reshape(devices, capacity))
+    requests = (digits[:devices] * 128.0 + digits[devices:]).astype(jnp.int32)
+    return slots.reshape(-1), requests
 
 
-def unpack_rows(returned, slot_index):
-    return returned[slot_index]
-
-
-def fetch_apart(owner, rows, features, devices):
-    capacity = (2 * owner.shape[0] + devices - 1) // devices
-    slot_index, requests = bucket_rows(owner, rows, devices, capacity)
-    arrived = lax.all_to_all(requests, "dom", split_axis=0, concat_axis=0, tiled=True)
-    located = features[arrived.reshape(-1)].reshape(devices, capacity, features.shape[1])
+def exchange(requests, features, devices):
+    capacity = requests.shape[1]
+    located = features[requests.reshape(-1)].reshape(devices, capacity, features.shape[1])
     returned = lax.all_to_all(located, "dom", split_axis=0, concat_axis=0, tiled=True)
-    return unpack_rows(returned.reshape(devices * capacity, features.shape[1]), slot_index)
+    return returned.reshape(devices * capacity, features.shape[1])
 
 
 def rgcn_layer(self_rows, neighbours, relations, weights):
@@ -78,9 +90,23 @@
     first_count = hop1_row.shape[0]
     positives = edge_mask.shape[0]
     blocks = positives // BLOCK
-    x_hop2 = fetch_apart(hop2_owner, hop2_row, features, devices)
-    x_hop1 = fetch_apart(hop1_owner, hop1_row, features, devices)
-    x_seed = fetch_apart(seed_owner, seed_row, features, devices)
+    second_count = hop2_row.shape[0]
+    caps = [
+        (2 * length + devices - 1) // devices for length in (second_count, first_count, seed_count)
+    ]
+    owners = jnp.concatenate([hop2_owner[:, 0], hop1_owner[:, 0], seed_owner[:, 0]])
+    rows = jnp.concatenate([hop2_row, hop1_row, seed_row])
+    sets = (second_count // seed_count, first_count // seed_count, 1)
+    slots, requests = bucket_all(owners, rows, seed_count, sets, caps, devices)
+    arrived = lax.all_to_all(requests, "dom", split_axis=0, concat_axis=0, tiled=True)
+    near = caps[0]
+    middle = caps[0] + caps[1]
+    got_hop2 = exchange(arrived[:, :near], features, devices)
+    got_hop1 = exchange(arrived[:, near:middle], features, devices)
+    got_seed = exchange(arrived[:, middle:], features, devices)
+    x_hop2 = got_hop2[slots[:second_count]]
+    x_hop1 = got_hop1[slots[second_count : second_count + first_count]]
+    x_seed = got_seed[slots[second_count + first_count :]]
     first_hop = jax.nn.relu(
         rgcn_layer(
             x_hop1,
@@ -117,7 +143,8 @@
     top_score = jnp.max(scores, axis=1, keepdims=True)
     edge_loss = top_score[:, 0] + jnp.log(jnp.sum(jnp.exp(scores - top_score), axis=1)) - positive
     weights = edge_mask.astype(jnp.float32)
-    loss_total, edge_total = lax.psum((jnp.sum(weights * edge_loss), jnp.sum(weights)), "dom")
+    sums = jnp.stack([jnp.sum(weights * edge_loss), jnp.sum(weights)])
+    loss_total, edge_total = jnp.sum(lax.all_gather(sums, "dom"), axis=0)
     mean_loss = loss_total / jnp.maximum(edge_total, 1.0)
     return (edge_loss, mean_loss)
 

time: 229 us -> 207 us (0.904)
  starting transfers between devices: 29.5 us -> 9.91 us
  blocking collectives: 38.4 us -> 52.4 us
  matrix products: 14.3 us -> 3.14 us
  waiting for transfers between devices: 51 us -> 45.1 us
    psum x1 -> x0, blocking collectives: 38.4 us -> none  [shards(): lax.psum((jnp.sum(weights * edge_loss), jnp.sum(weights)), 'dom')]
    unnamed x0 -> x1, blocking collectives: none -> 38 us
    all_to_all x6 -> x3, starting transfers between devices: 29.5 us -> 9.91 us  [exchange(): lax.all_to_all(located, 'dom', split_axis=0, concat_axis=0, tiled=True)]
    all_to_all x0 -> x1, blocking collectives: none -> 14.4 us  [shards(): lax.all_to_all(requests, 'dom', split_axis=0, concat_axis=0, tiled=True)]
    dot_general x6 -> x2, matrix products: 12.4 us -> 1.21 us  [the longest x1 0.81 us: bucket_all(): lax.dot_general(jnp.concatenate([high, low], axis=1), placed, (((0,), (0,...]
    all_to_all x6 -> x3, waiting for transfers between devices: 51 us -> 45.1 us  [exchange(): lax.all_to_all(located, 'dom', split_axis=0, concat_axis=0, tiled=True)]
    unnamed x52 -> x55, local copies, waits for them, and re-layouts: 7.83 us -> 9.93 us
  transfers between devices with their start and end apart: 6 -> 3, of which waited for: 4 -> 3; matrix products, arithmetic and copies ran while one was open for 33% -> 25% of each run, Pallas kernels for 0% -> 0%
where the time goes in v1:
time: 207 us; the launch traced here: 206 us
  local copies, waits for them, and re-layouts  75.4 us (36%)
  blocking collectives  52.4 us (25%)
  waiting for transfers between devices  45.1 us (22%)
  other arithmetic  16.3 us (8%)
  starting transfers between devices  9.91 us (5%)
  between operations  3.74 us (2%)
  matrix products  3.14 us (2%)
    all_to_all x3, waiting for transfers between devices, exchange(): lax.all_to_all(located, 'dom', split_axis=0, concat_axis=0, tiled=True)  45.1 us
    unnamed x1, blocking collectives  38 us
    gather x3, local copies, waits for them, and re-layouts, exchange(): features[requests.reshape(-1)].reshape(devices, capacity, features.shape[1])  33.1 us
    all_to_all x1, blocking collectives, shards(): lax.all_to_all(requests, 'dom', split_axis=0, concat_axis=0, tiled=True)  14.4 us
    unnamed x55, local copies, waits for them, and re-layouts  9.93 us
    all_to_all x3, starting transfers between devices, exchange(): lax.all_to_all(located, 'dom', split_axis=0, concat_axis=0, tiled=True)  9.91 us
    gather x1, local copies, waits for them, and re-layouts, shards(): x_hop2 = got_hop2[slots[:second_count]]  7.43 us
    mul x3, other arithmetic, rgcn_layer(): shares[:, 0, :, None] * neighbours[:, 0, None, :].astype(jnp.float32)  5.41 us
  transfers between devices with their start and end apart: 3, of which 3 were waited for; matrix products, arithmetic and copies ran while one was open for 25% of the time, Pallas kernels for 0%

profile of v1, /device:TPU:0, one launch (start us, length us, event | category | flops | bytes accessed | tf_op | source)
XLA Modules:
  0.0 206.0 jit_solution(11090021239525975405)
XLA Ops:
  0.7 0.8 reduce.2
  1.5 0.7 reduce.3
  2.2 0.7 reduce.4
  2.9 0.7 constant_dynamic-update-slice_fusion.2
  3.6 0.7 constant_dynamic-update-slice_fusion.1
  4.3 0.7 constant_dynamic-update-slice_fusion
  5.1 0.1 convert_reduce_fusion
  5.3 0.4 fusion.14
  6.0 0.8 fusion
  6.9 14.4 %all_to_all.27 = s32[32,1,234]{2,1,0:T(1,128)S(1)} all-to-all(s32[32,1,234]{2,1,0:T(1,128)S(1)} %copy.17), channel_id=1, replica_groups=mesh['dom'=32] {'dom'}, dimensions={0} | all-to-all | bytes 59904 | tf_op jit(solution)/shard_map/all_to_all | solution.py:101
  21.3 0.1 reshape.481
  21.5 6.6 %gather_fusion = bf16[576,256]{1,0:T(8,128)(2,1)S(1)} fusion(bf16[16384,256]{1,0:T(8,128)(2,1)} %param.14, s32[1024]{0:T(1024)S(1)} %pad_clamp_fusion.5), kind=kCustom, calls=%fused_computation | custom fusion | bytes 592128 | tf_op jit(solution)/shard_map/gather | solution.py:53
  28.1 0.8 reshape.482
  28.9 2.6 %all-to-all-start.1 = ((bf16[32,18,256]{2,1,0:T(8,128)(2,1)}), bf16[32,18,256]{2,1,0:T(8,128)(2,1)S(1)}, u32[]{:S(2)}, u32[]{:S(2)}) async-start(bf16[32,18,256]{2,1,0:T(8,128)(2,1)} %reshape.482), calls=%async_computation.1 | async-start | bytes 786432 | tf_op jit(solution)/shard_map/all_to_all | solution.py:54
  31.8 10.7 %gather_fusion.2 = bf16[2304,256]{1,0:T(8,128)(2,1)} fusion(bf16[16384,256]{1,0:T(8,128)(2,1)} %param.14, s32[3072]{0:T(1024)S(1)} %pad_clamp_fusion.2), kind=kCustom, calls=%fused_computation.2 | custom fusion | bytes 2368512 | tf_op jit(solution)/shard_map/gather | solution.py:53
  42.5 2.3 %all-to-all-done.1 = bf16[32,18,256]{2,1,0:T(8,128)(2,1)S(1)} async-done(((bf16[32,18,256]{2,1,0:T(8,128)(2,1)}), bf16[32,18,256]{2,1,0:T(8,128)(2,1)S(1)}, u32[]{:S(2)}, u32[]{:S(2)}) %all-to-all-start.1) | async-done | bytes 294944 | tf_op jit(solution)/shard_map/all_to_all | solution.py:54
  44.8 0.8 copy-done.5
  45.5 3.5 %all-to-all-start.2 = ((bf16[32,72,256]{2,1,0:T(8,128)(2,1)}), bf16[32,72,256]{2,1,0:T(8,128)(2,1)S(1)}, u32[]{:S(2)}, u32[]{:S(2)}) async-start(bf16[32,72,256]{2,1,0:T(8,128)(2,1)} %bitcast.5), calls=%async_computation.2 | async-start | bytes 2359296 | tf_op jit(solution)/shard_map/all_to_all | solution.py:54
  49.1 0.1 reshape.488
  49.2 15.8 %gather_fusion.4 = bf16[4608,256]{1,0:T(8,128)(2,1)} fusion(bf16[16384,256]{1,0:T(8,128)(2,1)} %param.14, s32[5120]{0:T(1024)S(1)} %pad_clamp_fusion), kind=kCustom, calls=%fused_computation.4 | custom fusion | bytes 4737024 | tf_op jit(solution)/shard_map/gather | solution.py:53
  65.1 13.0 %all-to-all-done.2 = bf16[32,72,256]{2,1,0:T(8,128)(2,1)S(1)} async-done(((bf16[32,72,256]{2,1,0:T(8,128)(2,1)}), bf16[32,72,256]{2,1,0:T(8,128)(2,1)S(1)}, u32[]{:S(2)}, u32[]{:S(2)}) %all-to-all-start.2) | async-done | bytes 1179680 | tf_op jit(solution)/shard_map/all_to_all | solution.py:54
  78.1 1.0 copy-done.1
  79.1 3.8 %all-to-all-start.3 = ((bf16[32,144,256]{2,1,0:T(8,128)(2,1)}), bf16[32,144,256]{2,1,0:T(8,128)(2,1)S(1)}, u32[]{:S(2)}, u32[]{:S(2)}) async-start(bf16[32,144,256]{2,1,0:T(8,128)(2,1)} %bitcast.80), calls=%async_computation.3 | async-start | bytes 4718592 | tf_op jit(solution)/shard_map/all_to_all | solution.py:54
  83.0 1.4 eq.89
  84.4 1.3 copy.23
  85.8 1.1 copy.24
  86.8 1.1 copy.25
  88.0 0.2 eq.85
  88.3 0.1 copy.19
  88.5 0.8 copy.20
  89.3 0.8 copy.21
  90.1 0.8 copy.22
  91.0 1.1 reshape.483
  92.1 2.5 %gather_fusion.1 = bf16[288,256]{1,0:T(8,128)(2,1)} fusion(bf16[576,256]{1,0:T(8,128)(2,1)S(1)} %reshape.483, s32[1024]{0:T(1024)S(1)} %pad_clamp_fusion.4), kind=kCustom, calls=%fused_computation.1 | custom fusion | bytes 296064 | tf_op jit(solution)/shard_map/gather | solution.py:109
  94.7 5.4 %gather_fusion.3 = bf16[1152,256]{1,0:T(8,128)(2,1)} fusion(bf16[2304,256]{1,0:T(8,128)(2,1)} %bitcast.79, s32[2048]{0:T(1024)S(1)} %pad_clamp_fusion.3), kind=kCustom, calls=%fused_computation.3 | custom fusion | bytes 1184256 | tf_op jit(solution)/shard_map/gather | solution.py:108
  100.0 2.3 %reshape.487 = bf16[288,4,256]{2,1,0:T(4,128)(2,1)} reshape(bf16[1152,256]{1,0:T(8,128)(2,1)} %gather_fusion.3) | data formatting | bytes 1179648 | tf_op jit(solution)/shard_map/reshape | solution.py:121
  102.3 2.9 %slice_convert_fusion.9 = (f32[288,1,256]{2,1,0:T(1,128)S(1)}, f32[288,1,256]{2,1,0:T(1,128)S(1)}, f32[288,1,256]{2,1,0:T(1,128)S(1)}, f32[288,1,256]{2,1,0:T(1,128)S(1)}) fusion(bf16[288,4,256]{2,1,0:T(4,128)(2,1)} %reshape.487), kind=kLoop, calls=%fused_computation.54 | loop fusion | flops 294912 | bytes 1769472 | tf_op jit(solution)/shard_map/mul | solution.py:63
  105.2 0.7 copy.58
  106.0 0.7 copy.59
  106.7 0.7 copy.60
  107.5 29.8 %all-to-all-done.3 = bf16[32,144,256]{2,1,0:T(8,128)(2,1)S(1)} async-done(((bf16[32,144,256]{2,1,0:T(8,128)(2,1)}), bf16[32,144,256]{2,1,0:T(8,128)(2,1)S(1)}, u32[]{:S(2)}, u32[]{:S(2)}) %all-to-all-start.3) | async-done | bytes 2359328 | tf_op jit(solution)/shard_map/all_to_all | solution.py:54
  137.2 7.4 %gather_fusion.5 = bf16[2304,256]{1,0:T(8,128)(2,1)} fusion(bf16[4608,256]{1,0:T(8,128)(2,1)S(1)} %bitcast.78, s32[3072]{0:T(1024)S(1)} %pad_clamp_fusion.1), kind=kCustom, calls=%fused_computation.5 | custom fusion | bytes 2368512 | tf_op jit(solution)/shard_map/gather | solution.py:107
  144.7 2.9 %reshape.491 = bf16[1152,2,256]{2,1,0:T(2,128)(2,1)S(1)} reshape(bf16[2304,256]{1,0:T(8,128)(2,1)} %gather_fusion.5) | data formatting | bytes 2359296 | tf_op jit(solution)/shard_map/reshape | solution.py:113
  147.5 1.7 slice_convert_fusion.1
  149.4 1.0 copy-done.2
  150.4 0.2 copy-done.3
  150.5 3.2 %add_convert_fusion = bf16[1152,4,256]{2,1,0:T(4,128)(2,1)S(1)} fusion(f32[1152,256]{1,0:T(8,128)S(1)} %bitcast.82, f32[1152,4]{1,0:T(8,128)S(1)} %copy-done.3, f32[1152,256]{1,0:T(8,128)S(1)} %bitcast.83, f32[1152,4]{1,0:T(8,128)S(1)} %copy-done.2), kind=kLoop, calls=%fused_computation.6 | loop fusion | flops 4718592 | bytes 4755456 | tf_op jit(solution)/shard_map/convert_element_type | solution.py:68
  153.8 0.6 copy.38
  154.4 0.5 copy-done.4
  154.8 1.0 fusion.8
  155.8 0.1 reshape.492
  155.9 0.8 slice_convert_fusion.5
  156.9 0.8 copy-done.6
  158.0 1.9 add_convert_fusion.2
  160.1 0.1 copy.39
  160.2 0.7 copy-done.12
  160.9 0.4 fusion.15
  161.3 0.4 fusion.19
  161.7 0.3 fusion.51
  161.9 0.1 fusion.30
  162.1 1.2 multiply_reduce_fusion
  163.3 1.5 maximum_dynamic-update-slice_fusion
  164.8 38.0 %all-reduce = f32[64]{0:T(128)S(1)} all-reduce(f32[64]{0:T(128)S(1)} %maximum_dynamic-update-slice_fusion), channel_id=2, replica_groups=mesh['dom'=32] {'dom'}, use_global_device_ids=true, to_apply=%add | all-reduce | flops 64 | bytes 512
  202.9 0.6 fusion.50
  (84 shorter events, 2.3 us)
Async XLA Ops:
  0.6 153.7 %copy-start = (bf16[1280,256]{1,0:T(8,128)(2,1)S(1)}, bf16[1280,256]{1,0:T(8,128)(2,1)}, u32[]{:S(2)}) copy-start(bf16[1280,256]{1,0:T(8,128)(2,1)} %param.15) | copy-start | bytes 1966084
  0.6 5.1 %copy-start.15 = (s32[13]{0:T(128)S(1)}, s32[13]{0:T(128)}, u32[]{:S(2)}) copy-start(s32[13]{0:T(128)} %constant.65.clone) | copy-start | bytes 160
  0.7 5.1 %copy-start.16 = (s32[13]{0:T(128)S(1)}, s32[13]{0:T(128)}, u32[]{:S(2)}) copy-start(s32[13]{0:T(128)} %constant.66.clone) | copy-start | bytes 160
  28.9 15.8 %all-to-all-start.1 = ((bf16[32,18,256]{2,1,0:T(8,128)(2,1)}), bf16[32,18,256]{2,1,0:T(8,128)(2,1)S(1)}, u32[]{:S(2)}, u32[]{:S(2)}) async-start(bf16[32,18,256]{2,1,0:T(8,128)(2,1)} %reshape.482), calls=%async_computation.1 | async-start | bytes 786432 | tf_op jit(solution)/shard_map/all_to_all | solution.py:54
  44.8 0.8 copy-start.5
  45.5 32.5 %all-to-all-start.2 = ((bf16[32,72,256]{2,1,0:T(8,128)(2,1)}), bf16[32,72,256]{2,1,0:T(8,128)(2,1)S(1)}, u32[]{:S(2)}, u32[]{:S(2)}) async-start(bf16[32,72,256]{2,1,0:T(8,128)(2,1)} %bitcast.5), calls=%async_computation.2 | async-start | bytes 2359296 | tf_op jit(solution)/shard_map/all_to_all | solution.py:54
  78.1 1.0 copy-start.1
  78.1 4.9 %copy-start.13 = (s32[2304]{0:T(1024)S(1)}, s32[2304]{0:T(1024)}, u32[]{:S(2)}) copy-start(s32[2304]{0:T(1024)} %param.24) | copy-start | bytes 27652
  79.1 58.1 %all-to-all-start.3 = ((bf16[32,144,256]{2,1,0:T(8,128)(2,1)}), bf16[32,144,256]{2,1,0:T(8,128)(2,1)S(1)}, u32[]{:S(2)}, u32[]{:S(2)}) async-start(bf16[32,144,256]{2,1,0:T(8,128)(2,1)} %bitcast.80), calls=%async_computation.3 | async-start | bytes 4718592 | tf_op jit(solution)/shard_map/all_to_all | solution.py:54
  83.0 5.0 %copy-start.14 = (s32[1152]{0:T(1024)S(1)}, s32[1152]{0:T(1024)}, u32[]{:S(2)}) copy-start(s32[1152]{0:T(1024)} %param.21) | copy-start | bytes 13828
  149.3 1.1 copy-start.2
  149.3 1.2 copy-start.3
  153.8 1.1 copy-start.4
  156.8 1.0 copy-start.6
  156.8 1.0 copy-start.7
  156.8 1.1 copy-start.8
  156.8 1.2 copy-start.9
  156.8 1.2 copy-start.10
  156.8 1.2 copy-start.11
  160.0 0.9 copy-start.12
  160.2 1.1 copy-start.18
  161.3 0.8 copy-start.17

commit v2 on v1

v2 whole, which is shorter than its diff:
```python
import functools

import jax
import jax.numpy as jnp
import numpy as np
from jax import lax
from jax.experimental import pallas as pl
from jax.experimental.pallas import tpu as pltpu
from jax.sharding import PartitionSpec as P

MESH = pl.DeviceIdType.MESH
HOP = 11
PIECE = 96
LANES = 128

R = 4
BLOCK = 128
NEG = 32
FAN1 = 4
FAN2 = 2


def round_up(value, multiple):
    return (value + multiple - 1) // multiple * multiple


def unroll_of(count):
    return max(step for step in range(1, 25) if count % step == 0)


def bucket_all(owners, rows, group, sets, caps, bases, strides, devices):
    blocks = owners.shape[0] // group
    onehot = owners[:, None] == jnp.arange(devices, dtype=jnp.int32)[None, :]
    hot = onehot.astype(jnp.bfloat16).reshape(blocks, group, devices)
    counter = jnp.arange(group, dtype=jnp.int32)
    earlier = (counter[:, None] > counter[None, :]).astype(jnp.bfloat16)
    prior = jnp.einsum("ij,bjd->bid", earlier, hot, preferred_element_type=jnp.float32)
    totals = jnp.sum(hot.astype(jnp.float32), axis=1)
    carry = []
    start = 0
    for count in sets:
        running = jnp.zeros((devices,), jnp.float32)
        for block in range(start, start + count):
            carry.append(running)
            running = running + totals[block]
        start += count
    prior = prior + jnp.stack(carry)[:, None, :]
    position = jnp.sum(prior * hot.astype(jnp.float32), axis=2).astype(jnp.int32)
    offsets = np.concatenate([[0], np.cumsum(caps)[:-1]])
    offset = jnp.asarray(np.repeat(offsets, sets), jnp.int32)
    base = jnp.asarray(np.repeat(np.asarray(bases), sets), jnp.int32)
    stride = jnp.asarray(np.repeat(np.asarray(strides), sets), jnp.int32)
    slots = owners.reshape(blocks, group) * stride[:, None] + base[:, None] + position
    place = (position + offset[:, None]).reshape(-1)
    width = round_up(sum(caps), LANES)
    placed = (place[:, None] == jnp.arange(width, dtype=jnp.int32)[None, :]).astype(jnp.bfloat16)
    high = jnp.where(onehot, (rows // 128)[:, None], 0).astype(jnp.bfloat16)
    low = jnp.where(onehot, (rows % 128)[:, None], 0).astype(jnp.bfloat16)
    digits = lax.dot_general(
        jnp.concatenate([high, low], axis=1),
        placed,
        (((0,), (0,)), ((), ())),
        preferred_element_type=jnp.float32,
    )
    requests = (digits[:devices] * 128.0 + digits[devices:]).astype(jnp.int32)
    return slots.reshape(-1), requests


def greet(devices, me):
    barrier = pltpu.get_barrier_semaphore()

    def hail(step, carry):
        other = lax.rem(me + step, devices)
        pl.semaphore_signal(barrier, inc=1, device_id=(other,), device_id_type=MESH)
        return carry

    lax.fori_loop(1, devices, hail, 0)
    pl.semaphore_wait(barrier, devices - 1)


def gather_rows(table, index_of, count, staging):
    step = unroll_of(count)

    def some(turn, carry):
        for lane in range(step):
            place = turn * step + lane
            staging[pl.ds(place, 1), :] = table[pl.ds(index_of(place), 1), :]
        return carry

    lax.fori_loop(0, count // step, some, 0)


def fetch_kernel(
    devices,
    caps,
    strides,
    requests,
    slots,
    features,
    far_out,
    near_out,
    table_half,
    table,
    arrived,
    wanted,
    far_send,
    near_send,
    far_recv,
    near_recv,
    far_table,
    near_table,
    staging,
    load_sem,
    small_sem,
    ask_send,
    ask_recv,
    far_send_sem,
    far_recv_sem,
    near_send_sem,
    near_recv_sem,
):
    me = lax.axis_index("dom")
    far_cap, near_cap = caps
    load = pltpu.make_async_copy(features, table_half, load_sem)
    load.start()
    greet(devices, me)

    def ask(turn, carry):
        other = lax.rem(me + turn * HOP, devices)
        pltpu.make_async_remote_copy(
            src_ref=requests.at[other],
            dst_ref=arrived.at[me],
            send_sem=ask_send,
            recv_sem=ask_recv,
            device_id=(other,),
            device_id_type=MESH,
        ).start()
        return carry

    lax.fori_loop(1, devices, ask, 0)
    own = pltpu.make_async_copy(requests.at[me], arrived.at[me], small_sem)
    own.start()
    load.wait()
    nodes = table.shape[0]
    chunk = nodes // 32

    def widen(turn, carry):
        where = pl.ds(pl.multiple_of(turn * chunk, chunk), chunk)
        table[where, :] = table_half[where, :].astype(jnp.float32)
        return carry

    lax.fori_loop(0, 32, widen, 0)
    own.wait()
    others = pl.ds(0, devices - 1)
    pltpu.make_async_copy(requests.at[others], arrived.at[others], ask_send).wait()
    pltpu.make_async_copy(requests.at[others], arrived.at[others], ask_recv).wait()
    move = pltpu.make_async_copy(arrived, wanted, small_sem)
    move.start()
    move.wait()

    def serve(first, cap, send, recv, send_sem, recv_sem):
        def pick(other):
            gather_rows(table, lambda place: wanted[other, 0, first + place], cap, staging)
            return staging[pl.ds(0, cap), :].astype(jnp.bfloat16)

        def one(turn, carry):
            other = lax.rem(me + turn * HOP, devices)
            send[other] = pick(other)
            pltpu.make_async_remote_copy(
                src_ref=send.at[other],
                dst_ref=recv.at[me],
                send_sem=send_sem,
                recv_sem=recv_sem,
                device_id=(other,),
                device_id_type=MESH,
            ).start()
            return carry

        lax.fori_loop(1, devices, one, 0)
        recv[me] = pick(me)

    serve(0, far_cap, far_send, far_recv, far_send_sem, far_recv_sem)
    serve(far_cap, near_cap, near_send, near_recv, near_send_sem, near_recv_sem)

    def settle(send, recv, recv_sem, cap, stride, wide, offset, out):
        pltpu.make_async_copy(send.at[others], recv.at[others], recv_sem).wait()

        def spread(source, carry):
            where = pl.ds(pl.multiple_of(source * stride, 8), cap)
            wide[where, :] = recv[source].astype(jnp.float32)
            return carry

        lax.fori_loop(0, devices, spread, 0)

        def piece(turn, carry):
            start = pl.multiple_of(turn * PIECE, PIECE)
            gather_rows(wide, lambda place: slots[offset + start + place], PIECE, staging)
            out[pl.ds(start, PIECE), :] = staging[pl.ds(0, PIECE), :].astype(jnp.bfloat16)
            return carry

        lax.fori_loop(0, out.shape[0] // PIECE, piece, 0)

    settle(far_send, far_recv, far_recv_sem, far_cap, strides[0], far_table, 0, far_out)
    settle(
        near_send,
        near_recv,
        near_recv_sem,
        near_cap,
        strides[1],
        near_table,
        far_out.shape[0],
        near_out,
    )
    pltpu.make_async_copy(far_send.at[others], far_recv.at[others], far_send_sem).wait()
    pltpu.make_async_copy(near_send.at[others], near_recv.at[others], near_send_sem).wait()


def fetch(requests, slots, features, caps, strides, counts, devices):
    nodes, width = features.shape
    far_cap, near_cap = caps
    asked = requests.shape[1]
    half, full = jnp.bfloat16, jnp.float32
    vmem = pl.BlockSpec(memory_space=pltpu.VMEM)
    return pl.pallas_call(
        functools.partial(fetch_kernel, devices, caps, strides),
        out_shape=[jax.ShapeDtypeStruct((count, width), half) for count in counts],
        in_specs=[
            vmem,
            pl.BlockSpec(memory_space=pltpu.SMEM),
            pl.BlockSpec(memory_space=pl.ANY),
        ],
        out_specs=[vmem, vmem],
        scratch_shapes=[
            pltpu.VMEM((nodes, width), half),
            pltpu.VMEM((nodes, width), full),
            pltpu.VMEM((devices, 1, asked), jnp.int32),
            pltpu.SMEM((devices, 1, asked), jnp.int32),
            pltpu.VMEM((devices, far_cap, width), half),
            pltpu.VMEM((devices, near_cap, width), half),
            pltpu.VMEM((devices, far_cap, width), half),
            pltpu.VMEM((devices, near_cap, width), half),
            pltpu.VMEM((devices * strides[0], width), full),
            pltpu.VMEM((devices * strides[1], width), full),
            pltpu.VMEM((round_up(max(far_cap, near_cap, PIECE), 8), width), full),
        ]
        + [pltpu.SemaphoreType.DMA(())] * 8,
        compiler_params=pltpu.CompilerParams(
            collective_id=0, has_side_effects=True, vmem_limit_bytes=60 * 1024 * 1024
        ),
        name="fetch",
    )(requests.reshape(devices, 1, asked), slots, features)


def total_kernel(devices, part, out, seen, send_sem, recv_sem):
    me = lax.axis_index("dom")
    greet(devices, me)

    def tell(turn, carry):
        other = lax.rem(me + turn * HOP, devices)
        pltpu.make_async_remote_copy(
            src_ref=part,
            dst_ref=seen.at[me],
            send_sem=send_sem,
            recv_sem=recv_sem,
            device_id=(other,),
            device_id_type=MESH,
        ).start()
        return carry

    lax.fori_loop(1, devices, tell, 0)
    seen[me] = part[...]
    others = pl.ds(0, devices - 1)
    pltpu.make_async_copy(seen.at[others], seen.at[others], recv_sem).wait()
    pltpu.make_async_copy(seen.at[others], seen.at[others], send_sem).wait()
    out[...] = jnp.sum(seen[...], axis=0)


def total_over(part, devices):
    return pl.pallas_call(
        functools.partial(total_kernel, devices),
        out_shape=jax.ShapeDtypeStruct(part.shape, part.dtype),
        in_specs=[pl.BlockSpec(memory_space=pltpu.VMEM)],
        out_specs=pl.BlockSpec(memory_space=pltpu.VMEM),
        scratch_shapes=[
            pltpu.VMEM((devices,) + part.shape, part.dtype),
            pltpu.SemaphoreType.DMA(()),
            pltpu.SemaphoreType.DMA(()),
        ],
        compiler_params=pltpu.CompilerParams(collective_id=1, has_side_effects=True),
        name="total",
    )(part)


def rgcn_layer(self_rows, neighbours, relations, weights):
    hot = [
        (relation[:, None] == jnp.arange(R, dtype=jnp.int32)[None, :]).astype(jnp.float32)
        for relation in relations
    ]
    tallies = jnp.maximum(sum(hot[1:], hot[0]), 1.0)
    wide = [neighbour.astype(jnp.float32) for neighbour in neighbours]
    means = []
    for kind in range(R):
        mean = (hot[0][:, kind] / tallies[:, kind])[:, None] * wide[0]
        for one, rows in zip(hot[1:], wide[1:]):
            mean = mean + (one[:, kind] / tallies[:, kind])[:, None] * rows
        means.append(mean.astype(jnp.bfloat16))
    inputs = jnp.concatenate([self_rows] + means, axis=1)
    return jnp.dot(inputs, weights, preferred_element_type=jnp.float32)


def shards(
    features,
    w_first,
    w_second,
    seed_owner,
    seed_row,
    hop1_owner,
    hop1_row,
    hop1_rel,
    hop2_owner,
    hop2_row,
    hop2_rel,
    edge_mask,
):
    devices = lax.axis_size("dom")
    width = features.shape[1]
    seed_count = seed_row.shape[0]
    first_count = hop1_row.shape[0]
    positives = edge_mask.shape[0]
    blocks = positives // BLOCK
    second_count = hop2_row.shape[0]
    caps = [
        (2 * length + devices - 1) // devices for length in (second_count, first_count, seed_count)
    ]
    near_cap = caps[1] + caps[2]
    strides = (round_up(caps[0], 8), round_up(near_cap, 8))

    def turned(values, fan):
        return values.reshape(-1, fan).T

    def hop2_order(values):
        return turned(values, FAN2).reshape(FAN2, seed_count, FAN1).swapaxes(1, 2).reshape(-1)

    def hop1_order(values):
        return turned(values, FAN1).reshape(-1)

    owners = jnp.concatenate(
        [hop2_order(hop2_owner[:, 0]), hop1_order(hop1_owner[:, 0]), seed_owner[:, 0]]
    )
    rows = jnp.concatenate([hop2_order(hop2_row), hop1_order(hop1_row), seed_row])
    sets = (second_count // seed_count, first_count // seed_count, 1)
    slots, requests = bucket_all(
        owners,
        rows,
        seed_count,
        sets,
        caps,
        (0, 0, caps[1]),
        (strides[0], strides[1], strides[1]),
        devices,
    )
    x_hop2, x_near = fetch(
        requests,
        slots,
        features,
        (caps[0], near_cap),
        strides,
        (second_count, first_count + seed_count),
        devices,
    )
    x_hop1 = x_near[:first_count]
    x_seed = x_near[first_count:]
    hop2_kinds = hop2_order(hop2_rel).reshape(FAN2, first_count)
    hop1_kinds = hop1_order(hop1_rel).reshape(FAN1, seed_count)
    first_hop = jax.nn.relu(
        rgcn_layer(
            x_hop1,
            [x_hop2[k * first_count : (k + 1) * first_count] for k in range(FAN2)],
            [hop2_kinds[k] for k in range(FAN2)],
            w_first,
        )
    ).astype(jnp.bfloat16)

    def by_seed(values):
        return [values[k * seed_count : (k + 1) * seed_count] for k in range(FAN1)]

    seed_kinds = [hop1_kinds[k] for k in range(FAN1)]
    first_seed = jax.nn.relu(
        rgcn_layer(x_seed, by_seed(x_hop1), seed_kinds, w_first)
    ).astype(jnp.bfloat16)
    second = rgcn_layer(first_seed, by_seed(first_hop), seed_kinds, w_second)
    sources = second[:positives]
    targets = second[positives : 2 * positives]
    negatives = second[2 * positives :].reshape(blocks, NEG, width)
    positive = jnp.sum(sources * targets, axis=1)
    negative = jnp.einsum(
        "bef,bqf->beq",
        sources.reshape(blocks, BLOCK, width),
        negatives,
        precision=lax.Precision.HIGHEST,
    ).reshape(positives, NEG)
    scores = jnp.concatenate([positive[:, None], negative], axis=1)
    top_score = jnp.max(scores, axis=1, keepdims=True)
    edge_loss = top_score[:, 0] + jnp.log(jnp.sum(jnp.exp(scores - top_score), axis=1)) - positive
    weights = edge_mask.astype(jnp.float32)
    lane = jnp.arange(LANES, dtype=jnp.int32)[None, :]
    part = jnp.where(lane == 0, jnp.sum(weights * edge_loss), 0.0)
    part = jnp.where(lane == 1, jnp.sum(weights), part)
    total = total_over(part, devices)
    loss_total, edge_total = total[0, 0], total[0, 1]
    mean_loss = loss_total / jnp.maximum(edge_total, 1.0)
    return (edge_loss, mean_loss)


def solution(mesh):
    placed = (
        P("dom", None),
        P(),
        P(),
        P("dom", None),
        P("dom"),
        P("dom", None),
        P("dom"),
        P("dom"),
        P("dom", None),
        P("dom"),
        P("dom"),
        P("dom"),
    )
    return jax.shard_map(
        shards, mesh=mesh, in_specs=placed, out_specs=(P("dom"), P()), check_vma=False
    )
```

time: 207 us -> 146 us (0.71)
  Pallas kernels: 0 us -> 116 us
  local copies, waits for them, and re-layouts: 75.4 us -> 9.88 us
  blocking collectives: 52.4 us -> 0 us
  waiting for transfers between devices: 45.1 us -> 0 us
  starting transfers between devices: 9.91 us -> 0 us
  other arithmetic: 16.3 us -> 11.1 us
    pallas_call x0 -> x2, Pallas kernels: none -> 116 us  [the longest x1 108 us: fetch(): pl.pallas_call(functools.partial(fetch_kernel, devices, caps, strides), o...]
    gather x6 -> x0, local copies, waits for them, and re-layouts: 48.5 us -> none  [the longest x3 33.1 us: exchange(): features[requests.reshape(-1)].reshape(devices, capacity, features.shape[1])]
    all_to_all x3 -> x0, waiting for transfers between devices: 45.1 us -> none  [exchange(): lax.all_to_all(located, 'dom', split_axis=0, concat_axis=0, tiled=True)]
    unnamed x1 -> x0, blocking collectives: 38 us -> none
    all_to_all x1 -> x0, blocking collectives: 14.4 us -> none  [shards(): lax.all_to_all(requests, 'dom', split_axis=0, concat_axis=0, tiled=True)]
    all_to_all x3 -> x0, starting transfers between devices: 9.91 us -> none  [exchange(): lax.all_to_all(located, 'dom', split_axis=0, concat_axis=0, tiled=True)]
    unnamed x55 -> x34, local copies, waits for them, and re-layouts: 9.93 us -> 2.58 us
    mul x3 -> x0, other arithmetic: 5.41 us -> none  [rgcn_layer(): shares[:, 0, :, None] * neighbours[:, 0, None, :].astype(jnp.float32)]
  transfers between devices with their start and end apart: 3 -> 0, of which waited for: 3 -> 0; matrix products, arithmetic and copies ran while one was open for 25% -> 0% of each run, Pallas kernels for 0% -> 0%
where the time goes in v2:
time: 146 us
  Pallas kernels  116 us (79%)
  other arithmetic  11.1 us (8%)
  local copies, waits for them, and re-layouts  9.88 us (7%)
  matrix products  5.02 us (3%)
  between operations  3.6 us (2%)
    pallas_call x1, Pallas kernels, fetch(): pl.pallas_call(functools.partial(fetch_kernel, devices, caps, strides), o...  108 us
    pallas_call x1, Pallas kernels, total_over(): pl.pallas_call(functools.partial(total_kernel, devices), out_shape=jax.Sh...  8.56 us
    unnamed x13, other arithmetic  5.2 us
    dot_general x3, matrix products, rgcn_layer(): return jnp.dot(inputs, weights, preferred_element_type=jnp.float32)  3.56 us

profile of v2, /device:TPU:0, one launch (start us, length us, event | category | flops | bytes accessed | tf_op | source)
XLA Modules:
  0.0 145.8 jit_solution(16868677662058498757)
XLA Ops:
  0.6 0.0 copy-start
  0.7 1.3 reshape.291
  2.0 0.3 copy.24
  2.3 0.1 concatenate.49
  2.4 0.2 reshape.293
  2.6 0.1 copy.25
  2.6 0.1 concatenate.50
  2.8 0.5 reshape_squeeze.6
  3.4 0.0 copy-start.14
  3.4 0.3 copy.22
  3.7 0.1 reshape.289
  3.8 0.2 reshape_squeeze.7
  4.0 0.1 copy.23
  4.1 0.1 reshape.290
  4.2 0.1 eq.187
  4.3 0.1 convert_reduce_fusion
  4.5 0.1 stack.2
  4.5 0.4 fusion.5
  5.0 0.1 convert_element_type.132
  5.0 0.1 add.220
  5.1 0.1 add.221
  5.2 0.0 copy-done.13
  5.2 0.1 add.224
  5.3 0.1 add.225
  5.4 0.0 copy-done.12
  5.4 0.1 mul.365
  5.4 0.1 mul.366
  5.5 0.6 add_add_fusion
  6.1 0.1 select_convert_fusion.1
  6.2 0.8 fusion
  7.0 0.6 reshape.294.requests
  7.7 107.6 %fetch.1 = (bf16[2304,256]{1,0:T(8,128)(2,1)}, bf16[1440,256]{1,0:T(8,128)(2,1)}) custom-call(s32[32,1,256]{2,1,0:T(1,128)} %reshape.294.requests, s32[3744]{0:T(1024)} %get-tuple-element.57.slots, bf16[16384,256]{1,0:T(8,128)(2,1)} %features.1), custom_call_target="tpu_custom_call" | custom-call | tf_op jit(solution)/shard_map/fetch/pallas_call | solution.py:224
  115.3 2.1 %slice_dynamic-update-slice_fusion = bf16[1152,1280]{1,0:T(8,128)(2,1)} fusion(bf16[1440,256]{1,0:T(8,128)(2,1)} %get-tuple-element.4), kind=kLoop, calls=%fused_computation.35 | loop fusion | bytes 1179648
  117.4 0.5 reshape.296
  117.9 0.3 copy.26
  118.2 0.1 eq.210
  118.3 0.1 eq.214
  118.4 0.1 fusion.88
  118.5 1.3 fusion.20
  119.8 1.3 fusion.19
  121.1 1.2 fusion.18
  122.3 1.2 fusion.17
  123.6 2.8 %fusion.1 = bf16[1152,256]{1,0:T(8,128)(2,1)S(1)} fusion(bf16[1152,1280]{1,0:T(8,128)(2,1)} %fusion.17, bf16[1280,256]{1,0:T(8,128)(2,1)S(1)} %copy-done), kind=kOutput, calls=%fused_computation.3 | convolution fusion | flops 755564544 | bytes 4194304 | tf_op jit(solution)/shard_map/dot_general | solution.py:308
  126.5 0.2 reshape.295
  126.6 0.4 slice_reduce_fusion.3
  127.1 0.1 fusion.102
  127.1 0.1 fusion.104
  127.2 0.2 fusion.66
  127.4 0.2 fusion.65
  127.7 0.2 fusion.64
  127.9 0.2 fusion.63
  128.1 0.4 fusion.15
  128.5 0.2 fusion.62
  128.7 0.2 fusion.61
  129.0 0.2 fusion.60
  129.2 0.2 fusion.59
  129.4 0.4 copy-done.3
  129.8 0.4 fusion.110
  130.2 0.3 fusion.109
  130.4 0.1 fusion.67
  130.6 1.1 convert_reduce_fusion.1
  131.7 1.8 %compare_select_fusion.1.part = f32[1,128]{1,0:T(1,128)} fusion(f32[]{:T(128)} %get-tuple-element.47, f32[]{:T(128)} %get-tuple-element.46), kind=kLoop, calls=%fused_computation.177 | loop fusion | flops 512 | bytes 520 | tf_op jit(solution)/shard_map/jit(_where)/select_n | solution.py:408
  133.5 8.6 %total.1 = f32[1,128]{1,0:T(1,128)} custom-call(f32[1,128]{1,0:T(1,128)} %compare_select_fusion.1.part), custom_call_target="tpu_custom_call" | custom-call | tf_op jit(solution)/shard_map/total/pallas_call | solution.py:279
  142.1 1.3 fusion.108
  (46 shorter events, 0.4 us)
Async XLA Ops:
  0.6 122.9 %copy-start = (bf16[1280,256]{1,0:T(8,128)(2,1)S(1)}, bf16[1280,256]{1,0:T(8,128)(2,1)}, u32[]{:S(2)}) copy-start(bf16[1280,256]{1,0:T(8,128)(2,1)} %param.16) | copy-start | bytes 1966084
  0.6 1.7 %copy-start.6 = (s32[1152]{0:T(1024)S(1)}, s32[1152]{0:T(1024)}, u32[]{:S(2)}) copy-start(s32[1152]{0:T(1024)} %param.21) | copy-start | bytes 13828
  0.7 2.1 %copy-start.9 = (s32[288]{0:T(512)S(1)}, s32[288]{0:T(512)}, u32[]{:S(2)}) copy-start(s32[288]{0:T(512)} %param.19) | copy-start | bytes 3460
  0.7 2.1 %copy-start.5 = (s32[2304,1]{0,1:T(1,128)S(1)}, s32[2304,1]{0,1:T(1,128)}, u32[]{:S(2)}) copy-start(s32[2304,1]{0,1:T(1,128)} %param.23) | copy-start | bytes 27652
  2.0 1.8 %copy-start.8 = (s32[1152,1]{0,1:T(1,128)S(1)}, s32[1152,1]{0,1:T(1,128)}, u32[]{:S(2)}) copy-start(s32[1152,1]{0,1:T(1,128)} %param.20) | copy-start | bytes 13828
  2.0 2.2 %copy-start.10 = (s32[288,1]{0,1:T(1,128)S(1)}, s32[288,1]{0,1:T(1,128)}, u32[]{:S(2)}) copy-start(s32[288,1]{0,1:T(1,128)} %param.18) | copy-start | bytes 3460
  3.4 1.7 %copy-start.14 = (s32[13]{0:T(128)S(1)}, s32[13]{0:T(128)}, u32[]{:S(2)}) copy-start(s32[13]{0:T(128)} %constant.54.clone) | copy-start | bytes 160
  3.4 1.8 %copy-start.13 = (s32[13]{0:T(128)S(1)}, s32[13]{0:T(128)}, u32[]{:S(2)}) copy-start(s32[13]{0:T(128)} %constant.55.clone) | copy-start | bytes 160
  3.4 2.0 %copy-start.12 = (s32[13]{0:T(128)S(1)}, s32[13]{0:T(128)}, u32[]{:S(2)}) copy-start(s32[13]{0:T(128)} %constant.56.clone) | copy-start | bytes 160
  115.3 2.1 %copy-start.4 = (s32[2304]{0:T(1024)S(1)}, s32[2304]{0:T(1024)}, u32[]{:S(2)}) copy-start(s32[2304]{0:T(1024)} %param.25) | copy-start | bytes 27652
  115.3 3.2 %copy-start.1 = (bf16[2304,256]{1,0:T(8,128)(2,1)S(1)}, bf16[2304,256]{1,0:T(8,128)(2,1)}, u32[]{:S(2)}) copy-start(bf16[2304,256]{1,0:T(8,128)(2,1)} %get-tuple-element.5) | copy-start | bytes 3538948
  123.6 2.8 %copy-start.2 = (bf16[1440,256]{1,0:T(8,128)(2,1)S(1)}, bf16[1440,256]{1,0:T(8,128)(2,1)}, u32[]{:S(2)}) copy-start(bf16[1440,256]{1,0:T(8,128)(2,1)} %get-tuple-element.4) | copy-start | bytes 2211844
  123.6 2.9 %copy-start.7 = (s32[1152]{0:T(1024)S(1)}, s32[1152]{0:T(1024)}, u32[]{:S(2)}) copy-start(s32[1152]{0:T(1024)} %param.22) | copy-start | bytes 13828
  128.7 1.1 copy-start.3
  129.8 0.8 copy-start.11

commit v3 on v2

--- a/solution.py
+++ b/solution.py
@@ -94,11 +94,17 @@
     devices,
     caps,
     strides,
+    counts,
     requests,
     slots,
     features,
-    far_out,
-    near_out,
+    w_first,
+    w_second,
+    far_kinds,
+    near_kinds,
+    mask,
+    loss_out,
+    mean_out,
     table_half,
     table,
     arrived,
@@ -110,6 +116,13 @@
     far_table,
     near_table,
     staging,
+    partial,
+    near_rows,
+    first_hop,
+    first_seed,
+    second,
+    part,
+    seen,
     load_sem,
     small_sem,
     ask_send,
@@ -118,8 +131,12 @@
     far_recv_sem,
     near_send_sem,
     near_recv_sem,
+    tell_send,
+    tell_recv,
 ):
     me = lax.axis_index("dom")
+    far_count, first_count, seed_count = counts
+    width = table.shape[1]
     far_cap, near_cap = caps
     load = pltpu.make_async_copy(features, table_half, load_sem)
     load.start()
@@ -182,7 +199,7 @@
     serve(0, far_cap, far_send, far_recv, far_send_sem, far_recv_sem)
     serve(far_cap, near_cap, near_send, near_recv, near_send_sem, near_recv_sem)
 
-    def settle(send, recv, recv_sem, cap, stride, wide, offset, out):
+    def settle(send, recv, recv_sem, cap, stride, wide):
         pltpu.make_async_copy(send.at[others], recv.at[others], recv_sem).wait()
 
         def spread(source, carry):
@@ -192,43 +209,152 @@
 
         lax.fori_loop(0, devices, spread, 0)
 
-        def piece(turn, carry):
-            start = pl.multiple_of(turn * PIECE, PIECE)
-            gather_rows(wide, lambda place: slots[offset + start + place], PIECE, staging)
-            out[pl.ds(start, PIECE), :] = staging[pl.ds(0, PIECE), :].astype(jnp.bfloat16)
-            return carry
-
-        lax.fori_loop(0, out.shape[0] // PIECE, piece, 0)
-
-    settle(far_send, far_recv, far_recv_sem, far_cap, strides[0], far_table, 0, far_out)
-    settle(
-        near_send,
-        near_recv,
-        near_recv_sem,
-        near_cap,
-        strides[1],
-        near_table,
-        far_out.shape[0],
-        near_out,
-    )
+    def weighed(values, kinds, weights):
+        fan = len(values)
+        hot = [
+            [(kinds[:, k : k + 1] == kind).astype(jnp.float32) for k in range(fan)]
+            for kind in range(R)
+        ]
+        result = None
+        for kind in range(R):
+            share = 1.0 / jnp.maximum(sum(hot[kind][1:], hot[kind][0]), 1.0)
+            mean = (hot[kind][0] * share) * values[0]
+            for k in range(1, fan):
+                mean = mean + (hot[kind][k] * share) * values[k]
+            term = jnp.dot(
+                mean.astype(jnp.bfloat16),
+                weights[(kind + 1) * width : (kind + 2) * width, :],
+                preferred_element_type=jnp.float32,
+            )
+            result = term if result is None else result + term
+        return result
+
+    def itself(values, weights):
+        return jnp.dot(
+            values.astype(jnp.bfloat16), weights[:width, :], preferred_element_type=jnp.float32
+        )
+
+    settle(far_send, far_recv, far_recv_sem, far_cap, strides[0], far_table)
+
+    def far_piece(turn, carry):
+        start = pl.multiple_of(turn * PIECE, PIECE)
+        values = []
+        for k in range(FAN2):
+            gather_rows(
+                far_table, lambda place: slots[k * first_count + start + place], PIECE, staging
+            )
+            values.append(staging[pl.ds(0, PIECE), :])
+        where = pl.ds(start, PIECE)
+        partial[where, :] = weighed(values, far_kinds[where, :], w_first)
+        return carry
+
+    lax.fori_loop(0, first_count // PIECE, far_piece, 0)
+    settle(near_send, near_recv, near_recv_sem, near_cap, strides[1], near_table)
+    gather_rows(
+        near_table, lambda place: slots[far_count + place], first_count + seed_count, near_rows
+    )
+
+    def hop_piece(turn, carry):
+        where = pl.ds(pl.multiple_of(turn * PIECE, PIECE), PIECE)
+        layer = itself(near_rows[where, :], w_first) + partial[where, :]
+        rounded = jnp.maximum(layer, 0.0).astype(jnp.bfloat16)
+        first_hop[where, :] = rounded.astype(jnp.float32)
+        return carry
+
+    lax.fori_loop(0, first_count // PIECE, hop_piece, 0)
+
+    def seed_layer(start, own_rows, own_start, rows, weights):
+        where = pl.ds(start, PIECE)
+        values = [
+            rows[pl.ds(pl.multiple_of(k * seed_count + start, PIECE), PIECE), :]
+            for k in range(FAN1)
+        ]
+        own_where = pl.ds(pl.multiple_of(own_start + start, PIECE), PIECE)
+        return itself(own_rows[own_where, :], weights) + weighed(
+            values, near_kinds[where, :], weights
+        )
+
+    def seed_piece(turn, carry):
+        start = pl.multiple_of(turn * PIECE, PIECE)
+        where = pl.ds(start, PIECE)
+        layer = seed_layer(start, near_rows, first_count, near_rows, w_first)
+        first_seed[where, :] = jnp.maximum(layer, 0.0).astype(jnp.bfloat16).astype(jnp.float32)
+        second[where, :] = seed_layer(start, first_seed, 0, first_hop, w_second)
+        return carry
+
+    lax.fori_loop(0, seed_count // PIECE, seed_piece, 0)
+
+    positives = mask.shape[0]
+    loss_sum = jnp.zeros((1, 1), jnp.float32)
+    edge_sum = jnp.zeros((1, 1), jnp.float32)
+    for block in range(positives // BLOCK):
+        span = slice(block * BLOCK, (block + 1) * BLOCK)
+        sources = second[span, :]
+        targets = second[positives + block * BLOCK : positives + (block + 1) * BLOCK, :]
+        first_neg = 2 * positives + block * NEG
+        negatives = second[first_neg : first_neg + NEG, :]
+        positive = jnp.sum(sources * targets, axis=1, keepdims=True)
+        negative = lax.dot_general(
+            sources,
+            negatives,
+            (((1,), (1,)), ((), ())),
+            precision=lax.Precision.HIGHEST,
+            preferred_element_type=jnp.float32,
+        )
+        top_score = jnp.maximum(positive, jnp.max(negative, axis=1, keepdims=True))
+        spread_sum = jnp.exp(positive - top_score) + jnp.sum(
+            jnp.exp(negative - top_score), axis=1, keepdims=True
+        )
+        edge_loss = top_score + jnp.log(spread_sum) - positive
+        loss_out[span, :] = edge_loss
+        counted = mask[span, :].astype(jnp.float32)
+        loss_sum = loss_sum + jnp.sum(counted * edge_loss, axis=0, keepdims=True)
+        edge_sum = edge_sum + jnp.sum(counted, axis=0, keepdims=True)
+    lane = lax.broadcasted_iota(jnp.int32, (1, LANES), 1)
+    part[...] = jnp.where(lane == 0, loss_sum, jnp.where(lane == 1, edge_sum, 0.0))
+
+    def tell(turn, carry):
+        other = lax.rem(me + turn * HOP, devices)
+        pltpu.make_async_remote_copy(
+            src_ref=part,
+            dst_ref=seen.at[me],
+            send_sem=tell_send,
+            recv_sem=tell_recv,
+            device_id=(other,),
+            device_id_type=MESH,
+        ).start()
+        return carry
+
+    lax.fori_loop(1, devices, tell, 0)
+    seen[me] = part[...]
     pltpu.make_async_copy(far_send.at[others], far_recv.at[others], far_send_sem).wait()
     pltpu.make_async_copy(near_send.at[others], near_recv.at[others], near_send_sem).wait()
-
-
-def fetch(requests, slots, features, caps, strides, counts, devices):
+    pltpu.make_async_copy(seen.at[others], seen.at[others], tell_recv).wait()
+    pltpu.make_async_copy(seen.at[others], seen.at[others], tell_send).wait()
+    total = jnp.sum(seen[...], axis=0)
+    mean_out[...] = total[:, 0:1] / jnp.maximum(total[:, 1:2], 1.0)
+
+
+def fetch(
+    requests, slots, features, w_first, w_second, kinds, mask, caps, strides, counts, devices
+):
     nodes, width = features.shape
     far_cap, near_cap = caps
     asked = requests.shape[1]
     half, full = jnp.bfloat16, jnp.float32
     vmem = pl.BlockSpec(memory_space=pltpu.VMEM)
     return pl.pallas_call(
-        functools.partial(fetch_kernel, devices, caps, strides),
-        out_shape=[jax.ShapeDtypeStruct((count, width), half) for count in counts],
+        functools.partial(fetch_kernel, devices, caps, strides, counts),
+        out_shape=[
+            jax.ShapeDtypeStruct(mask.shape, full),
+            jax.ShapeDtypeStruct((1, 1), full),
+        ],
         in_specs=[
             vmem,
             pl.BlockSpec(memory_space=pltpu.SMEM),
             pl.BlockSpec(memory_space=pl.ANY),
-        ],
+        ]
+        + [vmem] * 5,
         out_specs=[vmem, vmem],
         scratch_shapes=[
             pltpu.VMEM((nodes, width), half),
@@ -242,70 +368,29 @@
             pltpu.VMEM((devices * strides[0], width), full),
             pltpu.VMEM((devices * strides[1], width), full),
             pltpu.VMEM((round_up(max(far_cap, near_cap, PIECE), 8), width), full),
+            pltpu.VMEM((counts[1], width), full),
+            pltpu.VMEM((counts[1] + counts[2], width), full),
+            pltpu.VMEM((counts[1], width), full),
+            pltpu.VMEM((counts[2], width), full),
+            pltpu.VMEM((counts[2], width), full),
+            pltpu.VMEM((1, LANES), full),
+            pltpu.VMEM((devices, 1, LANES), full),
         ]
-        + [pltpu.SemaphoreType.DMA(())] * 8,
+        + [pltpu.SemaphoreType.DMA(())] * 10,
         compiler_params=pltpu.CompilerParams(
             collective_id=0, has_side_effects=True, vmem_limit_bytes=60 * 1024 * 1024
         ),
         name="fetch",
-    )(requests.reshape(devices, 1, asked), slots, features)
-
-
-def total_kernel(devices, part, out, seen, send_sem, recv_sem):
-    me = lax.axis_index("dom")
-    greet(devices, me)
-
-    def tell(turn, carry):
-        other = lax.rem(me + turn * HOP, devices)
-        pltpu.make_async_remote_copy(
-            src_ref=part,
-            dst_ref=seen.at[me],
-            send_sem=send_sem,
-            recv_sem=recv_sem,
-            device_id=(other,),
-            device_id_type=MESH,
-        ).start()
-        return carry
-
-    lax.fori_loop(1, devices, tell, 0)
-    seen[me] = part[...]
-    others = pl.ds(0, devices - 1)
-    pltpu.make_async_copy(seen.at[others], seen.at[others], recv_sem).wait()
-    pltpu.make_async_copy(seen.at[others], seen.at[others], send_sem).wait()
-    out[...] = jnp.sum(seen[...], axis=0)
-
-
-def total_over(part, devices):
-    return pl.pallas_call(
-        functools.partial(total_kernel, devices),
-        out_shape=jax.ShapeDtypeStruct(part.shape, part.dtype),
-        in_specs=[pl.BlockSpec(memory_space=pltpu.VMEM)],
-        out_specs=pl.BlockSpec(memory_space=pltpu.VMEM),
-        scratch_shapes=[
-            pltpu.VMEM((devices,) + part.shape, part.dtype),
-            pltpu.SemaphoreType.DMA(()),
-            pltpu.SemaphoreType.DMA(()),
-        ],
-        compiler_params=pltpu.CompilerParams(collective_id=1, has_side_effects=True),
-        name="total",
-    )(part)
-
-
-def rgcn_layer(self_rows, neighbours, relations, weights):
-    hot = [
-        (relation[:, None] == jnp.arange(R, dtype=jnp.int32)[None, :]).astype(jnp.float32)
-        for relation in relations
-    ]
-    tallies = jnp.maximum(sum(hot[1:], hot[0]), 1.0)
-    wide = [neighbour.astype(jnp.float32) for neighbour in neighbours]
-    means = []
-    for kind in range(R):
-        mean = (hot[0][:, kind] / tallies[:, kind])[:, None] * wide[0]
-        for one, rows in zip(hot[1:], wide[1:]):
-            mean = mean + (one[:, kind] / tallies[:, kind])[:, None] * rows
-        means.append(mean.astype(jnp.bfloat16))
-    inputs = jnp.concatenate([self_rows] + means, axis=1)
-    return jnp.dot(inputs, weights, preferred_element_type=jnp.float32)
+    )(
+        requests.reshape(devices, 1, asked),
+        slots,
+        features,
+        w_first,
+        w_second,
+        kinds[0],
+        kinds[1],
+        mask,
+    )
 
 
 def shards(
@@ -323,11 +408,8 @@
     edge_mask,
 ):
     devices = lax.axis_size("dom")
-    width = features.shape[1]
     seed_count = seed_row.shape[0]
     first_count = hop1_row.shape[0]
-    positives = edge_mask.shape[0]
-    blocks = positives // BLOCK
     second_count = hop2_row.shape[0]
     caps = [
         (2 * length + devices - 1) // devices for length in (second_count, first_count, seed_count)
@@ -359,57 +441,21 @@
         (strides[0], strides[1], strides[1]),
         devices,
     )
-    x_hop2, x_near = fetch(
+    far_kinds = hop2_rel.reshape(seed_count, FAN1, FAN2).swapaxes(0, 1).reshape(-1, FAN2)
+    edge_loss, mean_loss = fetch(
         requests,
         slots,
         features,
+        w_first,
+        w_second,
+        (far_kinds, hop1_rel.reshape(seed_count, FAN1)),
+        edge_mask[:, None],
         (caps[0], near_cap),
         strides,
-        (second_count, first_count + seed_count),
+        (second_count, first_count, seed_count),
         devices,
     )
-    x_hop1 = x_near[:first_count]
-    x_seed = x_near[first_count:]
-    hop2_kinds = hop2_order(hop2_rel).reshape(FAN2, first_count)
-    hop1_kinds = hop1_order(hop1_rel).reshape(FAN1, seed_count)
-    first_hop = jax.nn.relu(
-        rgcn_layer(
-            x_hop1,
-            [x_hop2[k * first_count : (k + 1) * first_count] for k in range(FAN2)],
-            [hop2_kinds[k] for k in range(FAN2)],
-            w_first,
-        )
-    ).astype(jnp.bfloat16)
-
-    def by_seed(values):
-        return [values[k * seed_count : (k + 1) * seed_count] for k in range(FAN1)]
-
-    seed_kinds = [hop1_kinds[k] for k in range(FAN1)]
-    first_seed = jax.nn.relu(
-        rgcn_layer(x_seed, by_seed(x_hop1), seed_kinds, w_first)
-    ).astype(jnp.bfloat16)
-    second = rgcn_layer(first_seed, by_seed(first_hop), seed_kinds, w_second)
-    sources = second[:positives]
-    targets = second[positives : 2 * positives]
-    negatives = second[2 * positives :].reshape(blocks, NEG, width)
-    positive = jnp.sum(sources * targets, axis=1)
-    negative = jnp.einsum(
-        "bef,bqf->beq",
-        sources.reshape(blocks, BLOCK, width),
-        negatives,
-        precision=lax.Precision.HIGHEST,
-    ).reshape(positives, NEG)
-    scores = jnp.concatenate([positive[:, None], negative], axis=1)
-    top_score = jnp.max(scores, axis=1, keepdims=True)
-    edge_loss = top_score[:, 0] + jnp.log(jnp.sum(jnp.exp(scores - top_score), axis=1)) - positive
-    weights = edge_mask.astype(jnp.float32)
-    lane = jnp.arange(LANES, dtype=jnp.int32)[None, :]
-    part = jnp.where(lane == 0, jnp.sum(weights * edge_loss), 0.0)
-    part = jnp.where(lane == 1, jnp.sum(weights), part)
-    total = total_over(part, devices)
-    loss_total, edge_total = total[0, 0], total[0, 1]
-    mean_loss = loss_total / jnp.maximum(edge_total, 1.0)
-    return (edge_loss, mean_loss)
+    return (edge_loss[:, 0], mean_loss[0, 0])
 
 
 def solution(mesh):

time: 146 us -> 139 us (0.952)
  other arithmetic: 11.1 us -> 4.53 us
  Pallas kernels: 116 us -> 121 us
  matrix products: 5.02 us -> 1.21 us
    pallas_call x2 -> x1, Pallas kernels: 116 us -> 121 us  [fetch(): pl.pallas_call(functools.partial(fetch_kernel, devices, caps, strides, co...]
    dot_general x4 -> x0, matrix products: 3.81 us -> none  [the longest x3 3.56 us: rgcn_layer(): return jnp.dot(inputs, weights, preferred_element_type=jnp.float32)]
    unnamed x13 -> x4, other arithmetic: 5.2 us -> 2.18 us
    unnamed x34 -> x14, local copies, waits for them, and re-layouts: 2.58 us -> 0.09 us
    select_n x1 -> x0, other arithmetic: 1.8 us -> none  [shards(): part = jnp.where(lane == 1, jnp.sum(weights), part)]
    slice x3 -> x0, local copies, waits for them, and re-layouts: 1.7 us -> none  [the longest x1 1.27 us: shards(): loss_total, edge_total = (total[0, 0], total[0, 1])]
    concatenate x3 -> x0, other arithmetic: 1.69 us -> none  [rgcn_layer(): inputs = jnp.concatenate([self_rows] + means, axis=1)]
    reshape x0 -> x2, local copies, waits for them, and re-layouts: none -> 1.5 us  [the longest x1 0.81 us: shards(): hop1_rel.reshape(seed_count, FAN1)]
where the time goes in v3:
time: 139 us
  Pallas kernels  121 us (87%)
  local copies, waits for them, and re-layouts  9.01 us (6%)
  other arithmetic  4.53 us (3%)
  between operations  2.57 us (2%)
    pallas_call x1, Pallas kernels, fetch(): pl.pallas_call(functools.partial(fetch_kernel, devices, caps, strides, co...  121 us

profile of v3, /device:TPU:0, one launch (start us, length us, event | category | flops | bytes accessed | tf_op | source)
XLA Modules:
  0.0 138.7 jit_solution(17201990057975136673)
XLA Ops:
  0.6 0.0 copy-start.5
  0.6 0.0 copy-start.4
  0.7 0.0 copy-start.3
  0.7 0.0 copy-start
  0.7 1.3 reshape.239
  1.9 0.3 copy.26
  2.2 0.1 concatenate.37
  2.3 0.9 reshape.241
  3.2 0.1 copy.27
  3.3 0.1 concatenate.38
  3.4 0.7 constant_dynamic-update-slice_fusion
  4.1 0.7 reduce
  4.8 0.5 reshape_squeeze.6
  5.4 0.0 copy-start.1
  5.4 0.0 copy-start.2
  5.4 0.3 copy.24
  5.7 0.1 reshape.237
  5.7 0.7 reduce.1
  6.5 0.2 reshape_squeeze.7
  6.6 0.1 copy.25
  6.7 0.1 reshape.238
  6.8 0.7 reduce.2
  7.6 0.1 eq.41
  7.6 0.1 convert_reduce_fusion
  7.8 0.1 stack.2
  7.9 0.4 fusion.4
  8.3 0.1 convert_element_type.35
  8.4 0.0 copy-done.5
  8.4 0.1 add.118
  8.4 0.1 add.119
  8.5 0.0 copy-done.4
  8.5 0.1 add.122
  8.6 0.1 add.123
  8.7 0.0 copy-done.3
  8.7 0.1 mul.23
  8.8 0.1 mul.24
  8.8 0.6 add_add_fusion
  9.5 0.1 select_convert_fusion.1
  9.5 0.8 fusion
  10.4 0.6 reshape.242.requests
  11.0 0.0 copy-done
  11.0 0.7 reshape.243
  11.7 0.8 copy.28
  12.6 0.0 copy-done.1
  12.6 0.8 reshape.245.near_kinds
  13.4 0.0 copy-done.2
  13.4 0.7 copy.29.mask
  14.1 121.3 %fetch.1 = (f32[128,1]{1,0:T(8,128)}, f32[1,1]{1,0:T(1,128)}) custom-call(s32[32,1,256]{2,1,0:T(1,128)} %reshape.242.requests, s32[3744]{0:T(1024)} %get-tuple-element.14.slots, bf16[16384,256]{1,0:T(8,128)(2,1)} %features.1, bf16[1280,256]{1,0:T(8,128)(2,1)} %w_first.1, bf16[1280,256]{1,0:T(8,128)(2,1)} %w_second.1, s32[1152,2]{1,0:T(8,128)} %bitcast.23, ...), custom_call_target="tpu_custom_call" | custom-call | tf_op jit(solution)/shard_map/fetch/pallas_call | solution.py:346
  135.5 1.5 %reduce.3 = f32[128]{0:T(128)} reduce(f32[128,1]{1,0:T(8,128)} %get-tuple-element.4, f32[]{:T(128)} %constant.46), dimensions={1}, to_apply=%get-tuple-element.4.reduce_sub_computation | reduce | bytes 1028 | tf_op jit(solution)/shard_map/fetch/pallas_call | solution.py:346
  (8 shorter events, 0.1 us)
Async XLA Ops:
  0.6 7.7 %copy-start.5 = (s32[13]{0:T(128)S(1)}, s32[13]{0:T(128)}, u32[]{:S(2)}) copy-start(s32[13]{0:T(128)} %constant.40.clone) | copy-start | bytes 160
  0.6 7.9 %copy-start.4 = (s32[13]{0:T(128)S(1)}, s32[13]{0:T(128)}, u32[]{:S(2)}) copy-start(s32[13]{0:T(128)} %constant.41.clone) | copy-start | bytes 160
  0.7 8.0 %copy-start.3 = (s32[13]{0:T(128)S(1)}, s32[13]{0:T(128)}, u32[]{:S(2)}) copy-start(s32[13]{0:T(128)} %constant.42.clone) | copy-start | bytes 160
  0.7 10.3 %copy-start = (s32[2304]{0:T(1024)S(1)}, s32[2304]{0:T(1024)}, u32[]{:S(2)}) copy-start(s32[2304]{0:T(1024)} %param.25) | copy-start | bytes 27652
  5.4 7.2 %copy-start.1 = (s32[1152]{0:T(1024)S(1)}, s32[1152]{0:T(1024)}, u32[]{:S(2)}) copy-start(s32[1152]{0:T(1024)} %param.22) | copy-start | bytes 13828
  5.4 8.0 %copy-start.2 = (s32[128]{0:T(128)S(1)}, s32[128]{0:T(128)}, u32[]{:S(2)}) copy-start(s32[128]{0:T(128)} %param.26) | copy-start | bytes 1540

commit v4 on v3

--- a/solution.py
+++ b/solution.py
@@ -12,6 +12,7 @@
 HOP = 11
 PIECE = 96
 LANES = 128
+LOADS = 8
 
 R = 4
 BLOCK = 128
@@ -138,8 +139,14 @@
     far_count, first_count, seed_count = counts
     width = table.shape[1]
     far_cap, near_cap = caps
-    load = pltpu.make_async_copy(features, table_half, load_sem)
-    load.start()
+    chunk = table.shape[0] // LOADS
+    loads = []
+    for turn in range(LOADS):
+        where = pl.ds(turn * chunk, chunk)
+        loads.append(
+            pltpu.make_async_copy(features.at[where], table_half.at[where], load_sem.at[turn])
+        )
+        loads[-1].start()
     greet(devices, me)
 
     def ask(turn, carry):
@@ -157,16 +164,17 @@
     lax.fori_loop(1, devices, ask, 0)
     own = pltpu.make_async_copy(requests.at[me], arrived.at[me], small_sem)
     own.start()
-    load.wait()
-    nodes = table.shape[0]
-    chunk = nodes // 32
-
-    def widen(turn, carry):
-        where = pl.ds(pl.multiple_of(turn * chunk, chunk), chunk)
-        table[where, :] = table_half[where, :].astype(jnp.float32)
-        return carry
-
-    lax.fori_loop(0, 32, widen, 0)
+    part_rows = chunk // 4
+    for turn in range(LOADS):
+        loads[turn].wait()
+
+        def widen(quarter, carry):
+            start = pl.multiple_of(turn * chunk + quarter * part_rows, part_rows)
+            where = pl.ds(start, part_rows)
+            table[where, :] = table_half[where, :].astype(jnp.float32)
+            return carry
+
+        lax.fori_loop(0, 4, widen, 0)
     own.wait()
     others = pl.ds(0, devices - 1)
     pltpu.make_async_copy(requests.at[others], arrived.at[others], ask_send).wait()
@@ -284,32 +292,36 @@
 
     lax.fori_loop(0, seed_count // PIECE, seed_piece, 0)
 
-    positives = mask.shape[0]
+    blocks = mask.shape[0]
+    positives = blocks * BLOCK
     loss_sum = jnp.zeros((1, 1), jnp.float32)
     edge_sum = jnp.zeros((1, 1), jnp.float32)
-    for block in range(positives // BLOCK):
-        span = slice(block * BLOCK, (block + 1) * BLOCK)
-        sources = second[span, :]
-        targets = second[positives + block * BLOCK : positives + (block + 1) * BLOCK, :]
-        first_neg = 2 * positives + block * NEG
-        negatives = second[first_neg : first_neg + NEG, :]
-        positive = jnp.sum(sources * targets, axis=1, keepdims=True)
-        negative = lax.dot_general(
-            sources,
-            negatives,
+
+    def pairs(left, right):
+        return lax.dot_general(
+            left,
+            right,
             (((1,), (1,)), ((), ())),
             precision=lax.Precision.HIGHEST,
             preferred_element_type=jnp.float32,
         )
-        top_score = jnp.maximum(positive, jnp.max(negative, axis=1, keepdims=True))
+
+    for block in range(blocks):
+        sources = second[block * BLOCK : (block + 1) * BLOCK, :]
+        targets = second[positives + block * BLOCK : positives + (block + 1) * BLOCK, :]
+        first_neg = 2 * positives + block * NEG
+        negatives = second[first_neg : first_neg + NEG, :]
+        positive = pairs(jnp.ones((8, width), jnp.float32), sources * targets)[0:1, :]
+        negative = pairs(negatives, sources)
+        top_score = jnp.maximum(positive, jnp.max(negative, axis=0, keepdims=True))
         spread_sum = jnp.exp(positive - top_score) + jnp.sum(
-            jnp.exp(negative - top_score), axis=1, keepdims=True
+            jnp.exp(negative - top_score), axis=0, keepdims=True
         )
         edge_loss = top_score + jnp.log(spread_sum) - positive
-        loss_out[span, :] = edge_loss
-        counted = mask[span, :].astype(jnp.float32)
-        loss_sum = loss_sum + jnp.sum(counted * edge_loss, axis=0, keepdims=True)
-        edge_sum = edge_sum + jnp.sum(counted, axis=0, keepdims=True)
+        loss_out[block : block + 1, :] = edge_loss
+        counted = mask[block : block + 1, :].astype(jnp.float32)
+        loss_sum = loss_sum + jnp.sum(counted * edge_loss, axis=1, keepdims=True)
+        edge_sum = edge_sum + jnp.sum(counted, axis=1, keepdims=True)
     lane = lax.broadcasted_iota(jnp.int32, (1, LANES), 1)
     part[...] = jnp.where(lane == 0, loss_sum, jnp.where(lane == 1, edge_sum, 0.0))
 
@@ -376,7 +388,8 @@
             pltpu.VMEM((1, LANES), full),
             pltpu.VMEM((devices, 1, LANES), full),
         ]
-        + [pltpu.SemaphoreType.DMA(())] * 10,
+        + [pltpu.SemaphoreType.DMA((LOADS,))]
+        + [pltpu.SemaphoreType.DMA(())] * 9,
         compiler_params=pltpu.CompilerParams(
             collective_id=0, has_side_effects=True, vmem_limit_bytes=60 * 1024 * 1024
         ),
@@ -449,13 +462,13 @@
         w_first,
         w_second,
         (far_kinds, hop1_rel.reshape(seed_count, FAN1)),
-        edge_mask[:, None],
+        edge_mask.reshape(-1, BLOCK),
         (caps[0], near_cap),
         strides,
         (second_count, first_count, seed_count),
         devices,
     )
-    return (edge_loss[:, 0], mean_loss[0, 0])
+    return (edge_loss.reshape(-1), mean_loss[0, 0])
 
 
 def solution(mesh):

time: 139 us -> 138 us (level)
  other arithmetic: 4.53 us -> 3.06 us
    pallas_call x1 -> x0, other arithmetic: 1.47 us -> none  [fetch(): pl.pallas_call(functools.partial(fetch_kernel, devices, caps, strides, co...]
where the time goes in v4:
time: 138 us; the launch traced here: 137 us
  Pallas kernels  121 us (88%)
  local copies, waits for them, and re-layouts  9.44 us (7%)
  other arithmetic  3.06 us (2%)
  between operations  2.51 us (2%)
    pallas_call x1, Pallas kernels, fetch(): pl.pallas_call(functools.partial(fetch_kernel, devices, caps, strides, co...  121 us

profile of v4, /device:TPU:0, one launch (start us, length us, event | category | flops | bytes accessed | tf_op | source)
XLA Modules:
  0.0 137.5 jit_solution(14328085081288824115)
XLA Ops:
  0.6 0.0 copy-start.4
  0.6 0.0 copy-start.3
  0.7 0.0 copy-start.2
  0.7 0.0 copy-start
  0.7 1.3 reshape.245
  1.9 0.3 copy.24
  2.2 0.1 concatenate.37
  2.3 0.9 reshape.247
  3.2 0.1 copy.25
  3.3 0.1 concatenate.38
  3.4 0.7 constant_dynamic-update-slice_fusion
  4.1 0.7 reduce
  4.8 0.5 reshape_squeeze.6
  5.4 0.0 copy-start.1
  5.4 0.3 copy.22
  5.6 0.1 reshape.243
  5.7 0.7 reduce.1
  6.5 0.2 reshape_squeeze.7
  6.6 0.1 copy.23
  6.7 0.1 reshape.244
  6.8 0.7 reduce.2
  7.5 0.1 eq.41
  7.6 0.1 convert_reduce_fusion
  7.8 0.1 stack.2
  7.8 0.4 fusion.4
  8.3 0.1 convert_element_type.35
  8.3 0.0 copy-done.4
  8.4 0.1 add.118
  8.4 0.1 add.119
  8.5 0.0 copy-done.3
  8.5 0.1 add.122
  8.6 0.1 add.123
  8.7 0.0 copy-done.2
  8.7 0.1 mul.23
  8.8 0.1 mul.24
  8.8 0.6 add_add_fusion
  9.4 0.1 select_convert_fusion.1
  9.5 0.8 fusion
  10.3 0.6 reshape.248.requests
  11.0 0.0 copy-done
  11.0 0.7 reshape.249
  11.7 0.8 copy.26
  12.5 0.0 copy-done.1
  12.5 0.8 reshape.251.near_kinds
  13.4 121.3 %fetch.1 = (f32[1,128]{1,0:T(1,128)}, f32[1,1]{1,0:T(1,128)}) custom-call(s32[32,1,256]{2,1,0:T(1,128)} %reshape.248.requests, s32[3744]{0:T(1024)} %get-tuple-element.14.slots, bf16[16384,256]{1,0:T(8,128)(2,1)} %features.1, bf16[1280,256]{1,0:T(8,128)(2,1)} %w_first.1, bf16[1280,256]{1,0:T(8,128)(2,1)} %w_second.1, s32[1152,2]{1,0:T(8,128)} %bitcast.27, ...), custom_call_target="tpu_custom_call" | custom-call | tf_op jit(solution)/shard_map/fetch/pallas_call | solution.py:358
  134.6 1.2 copy.32
  (8 shorter events, 0.1 us)
Async XLA Ops:
  0.6 7.7 %copy-start.4 = (s32[13]{0:T(128)S(1)}, s32[13]{0:T(128)}, u32[]{:S(2)}) copy-start(s32[13]{0:T(128)} %constant.40.clone) | copy-start | bytes 160
  0.6 7.9 %copy-start.3 = (s32[13]{0:T(128)S(1)}, s32[13]{0:T(128)}, u32[]{:S(2)}) copy-start(s32[13]{0:T(128)} %constant.41.clone) | copy-start | bytes 160
  0.7 8.0 %copy-start.2 = (s32[13]{0:T(128)S(1)}, s32[13]{0:T(128)}, u32[]{:S(2)}) copy-start(s32[13]{0:T(128)} %constant.42.clone) | copy-start | bytes 160
  0.7 10.3 %copy-start = (s32[2304]{0:T(1024)S(1)}, s32[2304]{0:T(1024)}, u32[]{:S(2)}) copy-start(s32[2304]{0:T(1024)} %param.25) | copy-start | bytes 27652
  5.4 7.2 %copy-start.1 = (s32[1152]{0:T(1024)S(1)}, s32[1152]{0:T(1024)}, u32[]{:S(2)}) copy-start(s32[1152]{0:T(1024)} %param.22) | copy-start | bytes 13828
